TPU v7x, 128 devices: a whole 4x4x4 slice. The times are simulated.
128 devices in a mesh: gx: 8 (over y, x_lo), pa: 16 (over x_hi, z, core).
Axes of the slice: x: 4 (x_hi: 2, x_lo: 2; x = x_hi * 2 + x_lo), y: 4, z: 4, core: 2. Of those that a mesh axis runs over, the one named last changes fastest.
Arguments:
- plastic: float32 [6, 128, 128, 128], P(None, 'gx', 'pa'), may hold values from -6 to 6
- offsets: float32 [3, 16, 32, 128], P(None, 'pa', 'gx'), may hold values from 0 to 1
- lines: float32 [3, 16, 32, 128], P(None, 'pa', 'gx'), may hold values from -3 to 3
- burgers: float32 [3, 16, 32, 128], P(None, 'pa', 'gx'), may hold values from -3.6 to 3.6
- counts: int32 [16, 32], P('pa', 'gx'), may hold values from 1 to 128, as said below
- voxels: int32 [16, 32, 128], P('pa', 'gx'), may hold values from 0 to 16383, as said below
Outputs:
- stress: float32 [6, 128, 128, 128], P(None, 'gx', 'pa')
- moved: float32 [3, 16, 32, 128], P(None, 'pa', 'gx')
Inputs may be any that keep to these rules, and one draw needn't show every extreme that they name: `counts`: each count is at least 1 and some cell holds 128 live segments. `voxels`: A segment of cell c lies in its device's block of 16 x 8 x 128 grid points: v = (x * 8 + y) * 128 + z with local plane x among the 4 planes of cell c % 4.
All inputs are finite; a program needn't handle non-finite values.
Results may differ from a plain program's by a relative error of at most 0.0003.
Values sent between devices are 32-bit elements; how exact they have to be, the bound alone decides.
A program may use at most 64 MiB of HBM per device.

v0:
```python
import math

import jax
import jax.numpy as jnp
import numpy as np
from jax import lax
from jax.experimental import pallas as pl
from jax.experimental.pallas import tpu as pltpu
from jax.sharding import PartitionSpec as P

MESH = pl.DeviceIdType.MESH
F32 = jnp.float32
BF16 = jnp.bfloat16
N = 128
SLOTS = 32
CHUNKS = 3
CELLS = 4
HALO = 3
WIDE = CELLS + 2 * HALO

lame_lambda = 1.5
shear_modulus = 1.0
green_coef = 2.5 / 3.5
core_square = 0.09
pair_factor = 1.0 / (4.0 * math.pi)
step_size = 0.05
full_index = ((0, 5, 4), (5, 1, 3), (4, 3, 2))


def split_table(table):
    table = jnp.asarray(table, F32)
    high = table.astype(BF16)
    low = (table - high.astype(F32)).astype(BF16)
    return high, low


def np_split(table):
    table = np.asarray(table, np.float32)
    high = table.astype(jnp.bfloat16)
    low = (table - high.astype(np.float32)).astype(jnp.bfloat16)
    return high, low


def tables():
    index = np.arange(N)
    angle = 2.0 * np.pi * (np.outer(index, index) % N) / N
    cos, sin = np.cos(angle), np.sin(angle)
    lane = np.arange(N)
    bins = (lane // 4) * 2 + lane % 2
    part = (lane // 2) % 2
    ahead_z = np.where(part[None, :] == 0, cos[:, bins], -sin[:, bins])
    ahead_z = np.where((bins == 0)[None, :] & (part == 1)[None, :], cos[:, 64][:, None], ahead_z)
    weight = np.where(bins == 0, 1.0, 2.0) / N
    back_z = ahead_z.T * weight[:, None]
    ahead_y = np.concatenate([cos, sin], axis=1)
    back_y = np.concatenate([cos, -sin], axis=1) / N
    plane = ((lane % 4) * 2 + lane // 64) * 16 + (lane // 4) % 16
    cx, sx = cos[plane, :], sin[plane, :]
    ahead_x = np.block([[cx, -sx], [sx, cx]])
    back_x = np.block([[cx.T, sx.T], [-sx.T, cx.T]]) / N
    out = []
    high, low = np_split(ahead_z)
    zero = np.zeros_like(low)
    out.append(np.block([[high, low], [high, zero]]))
    high, low = np_split(back_z)
    out.append(np.block([[high, low], [high, zero]]))
    for table in (ahead_y, back_y):
        high, low = np_split(table)
        out.append(np.concatenate([high, low], axis=0))
    for table in (ahead_x, back_x):
        out.extend(np_split(table))
    return np.stack(out)


def split(value):
    high = value.astype(BF16)
    low = (value - high.astype(F32)).astype(BF16)
    return high, low


def dot(a, b):
    return lax.dot_general(a, b, (((1,), (0,)), ((), ())), preferred_element_type=F32)


def exchange_bits(first, second, shift, lane_bit):
    new_first = jnp.where(lane_bit, pltpu.roll(second, shift, 1), first)
    new_second = jnp.where(lane_bit, second, pltpu.roll(first, N - shift, 1))
    return new_first, new_second


def butterfly(tiles, lane):
    step = SLOTS // 2
    while step >= 1:
        bit = (lane & (step * 4)) != 0
        for index in range(SLOTS):
            if index & step == 0:
                tiles[index], tiles[index + step] = exchange_bits(
                    tiles[index], tiles[index + step], step * 4, bit
                )
        step //= 2
    return tiles


def turned(value, lane):
    return jnp.where((lane & 2) == 0, pltpu.roll(value, N - 2, 1), -pltpu.roll(value, 2, 1))


def z_matmul(rows, table):
    high, low = split(rows)
    both = dot(jnp.concatenate([high, low], axis=1), table)
    return both[:, :N] + both[:, N:]


def y_matmul(first, second, table, lane):
    top = jnp.concatenate([first, second], axis=1)
    low_half = jnp.concatenate([turned(first, lane), turned(second, lane)], axis=1)
    high, low = split(jnp.concatenate([top, low_half], axis=0))
    both = dot(table, high)
    return both[:N] + both[N:] + dot(table[:N], low)


def x_matmul(rows, table_high, table_low):
    count = rows.shape[0]
    high, low = split(rows)
    both = dot(jnp.concatenate([high, low], axis=0), table_high)
    return both[:count] + both[count:] + dot(high, table_low)


def stress_terms(strain, freq_x, freq_y, freq_z):
    xx, yy, zz, yz, xz, xy = strain
    trace = xx + yy + zz
    tau_xx = lame_lambda * trace + 2.0 * shear_modulus * xx
    tau_yy = lame_lambda * trace + 2.0 * shear_modulus * yy
    tau_zz = lame_lambda * trace + 2.0 * shear_modulus * zz
    tau_yz = 2.0 * shear_modulus * yz
    tau_xz = 2.0 * shear_modulus * xz
    tau_xy = 2.0 * shear_modulus * xy
    norm_x = tau_xx * freq_x + tau_xy * freq_y + tau_xz * freq_z
    norm_y = tau_xy * freq_x + tau_yy * freq_y + tau_yz * freq_z
    norm_z = tau_xz * freq_x + tau_yz * freq_y + tau_zz * freq_z
    square = freq_x * freq_x + freq_y * freq_y + freq_z * freq_z
    inverse = 1.0 / jnp.maximum(square, 1.0)
    along = (freq_x * norm_x + freq_y * norm_y + freq_z * norm_z) * inverse * inverse * green_coef
    half = inverse / (2.0 * shear_modulus)

    def term(first_q, second_q, first_n, second_n, plastic):
        total = (first_q * second_n + second_q * first_n) * half - first_q * second_q * along
        return total - plastic

    el_xx = term(freq_x, freq_x, norm_x, norm_x, xx)
    el_yy = term(freq_y, freq_y, norm_y, norm_y, yy)
    el_zz = term(freq_z, freq_z, norm_z, norm_z, zz)
    el_yz = term(freq_y, freq_z, norm_y, norm_z, yz)
    el_xz = term(freq_x, freq_z, norm_x, norm_z, xz)
    el_xy = term(freq_x, freq_y, norm_x, norm_y, xy)
    el_trace = el_xx + el_yy + el_zz
    return (
        lame_lambda * el_trace + 2.0 * shear_modulus * el_xx,
        lame_lambda * el_trace + 2.0 * shear_modulus * el_yy,
        lame_lambda * el_trace + 2.0 * shear_modulus * el_zz,
        2.0 * shear_modulus * el_yz,
        2.0 * shear_modulus * el_xz,
        2.0 * shear_modulus * el_xy,
    )


def signed_frequency(index):
    value = jnp.where(index < N // 2, index, jnp.where(index == N // 2, 0, index - N))
    return value.astype(F32)


def kernel(
    plastic_ref, table_hbm, offsets_ref, lines_ref, burgers_ref, counts_ref, voxels_ref,
    stress_ref, moved_ref,
    plastic_buf, table_buf, out1, in1, out2, in2, spec, out3, in3, out4, in4, stress_buf,
    seg, samp, lbuf, mbuf, pair_out,
    load_sem, send1, recv1, send2, recv2, send3, recv3, send4, recv4,
    halo_send, halo_recv, samp_send, samp_recv, store_sem,
):
    gx = lax.axis_index("gx")
    pa = lax.axis_index("pa")
    quarter = gx // 2
    x_low = gx % 2
    slot = x_low * 16 + pa
    left = {"gx": (gx + 7) % 8}
    right = {"gx": (gx + 1) % 8}
    cross = {"gx": (gx + 8 + 2 * x_low - 1) % 8}

    loads = [
        pltpu.make_async_copy(plastic_ref.at[pl.ds(2 * j, 2)], plastic_buf.at[pl.ds(2 * j, 2)], load_sem.at[j])
        for j in range(CHUNKS)
    ]
    table_loads = [
        pltpu.make_async_copy(table_hbm.at[i], table_buf.at[i], load_sem.at[CHUNKS + i]) for i in range(8)
    ]
    loads[0].start()
    table_loads[0].start()
    loads[1].start()
    loads[2].start()
    for i in (2, 4, 5, 6, 7, 3, 1):
        table_loads[i].start()

    def group_device(other):
        return {"gx": 2 * quarter + other // 16, "pa": other % 16}

    barrier = pltpu.get_barrier_semaphore()

    def greet(i, carry):
        pl.semaphore_signal(barrier, inc=1, device_id=group_device((slot + i) % SLOTS), device_id_type=MESH)
        return carry

    lax.fori_loop(1, SLOTS, greet, 0)
    for i in range(1, 4):
        pl.semaphore_signal(barrier, inc=1, device_id={"gx": (gx + 2 * i) % 8}, device_id_type=MESH)
    pl.semaphore_signal(barrier, inc=1, device_id=cross, device_id_type=MESH)

    lane8 = lax.broadcasted_iota(jnp.int32, (8, N), 1)
    lane32 = lax.broadcasted_iota(jnp.int32, (32, N), 1)
    lane128 = lax.broadcasted_iota(jnp.int32, (N, N), 1)

    def group_send(j, source, target, send_sem, recv_sem):
        def one(i, carry):
            other = (slot + i) % SLOTS
            pltpu.make_async_remote_copy(
                src_ref=source.at[j, other], dst_ref=target.at[j, slot],
                send_sem=send_sem.at[j], recv_sem=recv_sem.at[j],
                device_id=group_device(other), device_id_type=MESH,
            ).start()
            return carry

        lax.fori_loop(1, SLOTS, one, 0)
        pltpu.make_async_copy(source.at[j, slot], target.at[j, slot], recv_sem.at[j]).start()

    for j in range(CHUNKS):
        if j == 0:
            table_loads[0].wait()
        loads[j].wait()
        rows = plastic_buf[2 * j : 2 * j + 2].reshape(256, N)
        result = z_matmul(rows, table_buf[0])
        tiles = butterfly([result[8 * t : 8 * t + 8] for t in range(SLOTS)], lane8)
        for t in range(SLOTS):
            out1[j, t] = tiles[t]
        if j == 0:
            pl.semaphore_wait(barrier, 35)
        group_send(j, out1, in1, send1, recv1)

    counts = counts_ref[...]
    index = lax.broadcasted_iota(jnp.int32, (CELLS, N), 1)
    live = (index < counts.reshape(CELLS, 1)).astype(F32)
    first_position = []
    for k in range(3):
        value = offsets_ref[k, 0] - 0.5
        seg[HALO : HALO + CELLS, k, :] = value
        seg[HALO : HALO + CELLS, 3 + k, :] = lines_ref[k, 0]
        seg[HALO : HALO + CELLS, 6 + k, :] = burgers_ref[k, 0] * live
    to_left = pltpu.make_async_remote_copy(
        src_ref=seg.at[pl.ds(HALO, HALO)], dst_ref=seg.at[pl.ds(HALO + CELLS, HALO)],
        send_sem=halo_send.at[0], recv_sem=halo_recv.at[0], device_id=left, device_id_type=MESH,
    )
    to_right = pltpu.make_async_remote_copy(
        src_ref=seg.at[pl.ds(CELLS, HALO)], dst_ref=seg.at[pl.ds(0, HALO)],
        send_sem=halo_send.at[1], recv_sem=halo_recv.at[1], device_id=right, device_id_type=MESH,
    )
    to_left.start()
    to_right.start()

    to_left.wait()
    to_right.wait()
    line = [seg[:, 3 + k, :] for k in range(3)]
    burg = [seg[:, 6 + k, :] for k in range(3)]
    start = [seg[:, k, :] for k in range(3)]
    lbuf[...] = jnp.zeros_like(lbuf)
    mbuf[...] = jnp.zeros_like(mbuf)
    for c in range(3):
        for b in range(3):
            lbuf[:, 3 * c + b, :] = line[c] * burg[b]

    def pair_field(position, low, high):
        arm = [
            position[1] * line[2] - position[2] * line[1],
            position[2] * line[0] - position[0] * line[2],
            position[0] * line[1] - position[1] * line[0],
        ]
        for shift in range(3):
            moved_arm = [
                arm[0],
                arm[1] - (shift - 1.0) * line[2],
                arm[2] + (shift - 1.0) * line[1],
            ]
            for a in range(3):
                for b in range(3):
                    mbuf[shift, :, 3 * a + b, :] = moved_arm[a] * burg[b]
        pad = jnp.zeros((16 - WIDE, N), F32)
        columns = [jnp.transpose(jnp.concatenate([value, pad], axis=0)) for value in position]
        for cell in range(low, high):
            target = [value[cell : cell + 1] for value in position]
            weights, factors = [], []
            for shift in range(3):
                source = cell + shift - 1
                delta = [
                    target[k] - (shift - 1.0) * (k == 0) - columns[k][:, source : source + 1] for k in range(3)
                ]
                radius = delta[0] * delta[0] + delta[1] * delta[1] + delta[2] * delta[2] + core_square
                root = lax.rsqrt(radius)
                weights.append(root * root * root)
                factors.append(jnp.concatenate([lbuf[source], mbuf[shift, source]], axis=0))
            weight_high, weight_low = split(jnp.concatenate(weights, axis=0))
            factor_high, factor_low = split(jnp.concatenate(factors, axis=1))
            both = dot(jnp.concatenate([factor_high, factor_low], axis=0), weight_high)
            pair_out[cell] = both[:32] + both[32:] + dot(factor_high, weight_low)
        spread = [[pair_out[:, 3 * c + b, :] for b in range(3)] for c in range(3)]
        offset = [[pair_out[:, 16 + 3 * a + b, :] for b in range(3)] for a in range(3)]
        moment = [[None] * 3 for _ in range(3)]
        for b in range(3):
            for a in range(3):
                n, m = (a + 1) % 3, (a + 2) % 3
                moment[a][b] = position[n] * spread[m][b] - position[m] * spread[n][b] - offset[a][b]
        return [
            pair_factor * (moment[a][b] + moment[b][a])
            for a, b in ((0, 0), (1, 1), (2, 2), (1, 2), (0, 2), (0, 1))
        ]

    pair_out[...] = jnp.zeros_like(pair_out)
    field = pair_field(start, 1, WIDE - 1)

    for j in range(CHUNKS):
        pltpu.make_async_copy(in1.at[j], in1.at[j], recv1.at[j]).wait()
        if j == 0:
            table_loads[2].wait()
        result = y_matmul(
            in1[j, 0:16].reshape(N, N), in1[j, 16:32].reshape(N, N), table_buf[2], lane128
        )
        for low in range(2):
            out2[j, :, low] = result[:, N * low : N * low + N].reshape(4, 32, N)
        for i in range(1, 4):
            other = (quarter + i) % 4
            pltpu.make_async_remote_copy(
                src_ref=out2.at[j, other], dst_ref=in2.at[j, quarter],
                send_sem=send2.at[j], recv_sem=recv2.at[j],
                device_id={"gx": 2 * other + x_low}, device_id_type=MESH,
            ).start()
        pltpu.make_async_copy(out2.at[j, quarter], in2.at[j, quarter], recv2.at[j]).start()

    high_bit = (lane32 & 64) != 0
    part_bit = (lane32 & 2) != 0
    bin_bit = (lane32 & 1) != 0
    for j in range(CHUNKS):
        pltpu.make_async_copy(in2.at[j], in2.at[j], recv2.at[j]).wait()
        if j == 0:
            table_loads[4].wait()
            table_loads[5].wait()
        grid = [[in2[j, q, low] for low in range(2)] for q in range(4)]
        for q in range(4):
            grid[q][0], grid[q][1] = exchange_bits(grid[q][0], grid[q][1], 64, high_bit)
        for c in range(2):
            for q in range(2):
                grid[q][c], grid[q + 2][c] = exchange_bits(grid[q][c], grid[q + 2][c], 2, part_bit)
            for q in (0, 2):
                grid[q][c], grid[q + 1][c] = exchange_bits(grid[q][c], grid[q + 1][c], 1, bin_bit)
        rows = jnp.concatenate(
            [
                jnp.concatenate([grid[b][c], grid[2 + b][c]], axis=1)
                for c in range(2)
                for b in range(2)
            ],
            axis=0,
        )
        spec[2 * j : 2 * j + 2] = x_matmul(rows, table_buf[4], table_buf[5]).reshape(2, 2, 32, 2 * N)

    k_index = lax.broadcasted_iota(jnp.int32, (8, 2 * N), 1) % N
    freq_x = signed_frequency(k_index)
    for b in range(2):
        freq_z = (2 * slot + b).astype(F32)
        for t in range(4):
            row = lax.broadcasted_iota(jnp.int32, (8, 2 * N), 0) + 32 * quarter + 8 * t
            freq_y = signed_frequency(row)
            strain = [spec[c, b, 8 * t : 8 * t + 8, :] for c in range(6)]
            result = stress_terms(strain, freq_x, freq_y, freq_z)
            for c in range(6):
                spec[c, b, 8 * t : 8 * t + 8, :] = result[c]

    for j in range(CHUNKS):
        if j == 0:
            table_loads[6].wait()
            table_loads[7].wait()
        result = x_matmul(spec[2 * j : 2 * j + 2].reshape(N, 2 * N), table_buf[6], table_buf[7])
        grid = [[None, None] for _ in range(4)]
        for c in range(2):
            for b in range(2):
                at = 32 * (2 * c + b)
                grid[b][c] = result[at : at + 32, :N]
                grid[2 + b][c] = result[at : at + 32, N:]
        for c in range(2):
            for q in range(2):
                grid[q][c], grid[q + 2][c] = exchange_bits(grid[q][c], grid[q + 2][c], 2, part_bit)
            for q in (0, 2):
                grid[q][c], grid[q + 1][c] = exchange_bits(grid[q][c], grid[q + 1][c], 1, bin_bit)
        for q in range(4):
            grid[q][0], grid[q][1] = exchange_bits(grid[q][0], grid[q][1], 64, high_bit)
            for low in range(2):
                out3[j, q, low] = grid[q][low]
        for i in range(1, 4):
            other = (quarter + i) % 4
            pltpu.make_async_remote_copy(
                src_ref=out3.at[j, other], dst_ref=in3.at[j, quarter],
                send_sem=send3.at[j], recv_sem=recv3.at[j],
                device_id={"gx": 2 * other + x_low}, device_id_type=MESH,
            ).start()
        pltpu.make_async_copy(out3.at[j, quarter], in3.at[j, quarter], recv3.at[j]).start()

    for j in range(CHUNKS):
        pltpu.make_async_copy(in3.at[j], in3.at[j], recv3.at[j]).wait()
        if j == 0:
            table_loads[3].wait()
        result = y_matmul(
            in3[j, :, 0].reshape(N, N), in3[j, :, 1].reshape(N, N), table_buf[3], lane128
        )
        for low in range(2):
            out4[j, 16 * low : 16 * low + 16] = result[:, N * low : N * low + N].reshape(16, 8, N)
        group_send(j, out4, in4, send4, recv4)

    voxels = voxels_ref[0]
    row_of = (voxels >> 7) & 31
    z_of = voxels & 127
    sublane = lax.broadcasted_iota(jnp.int32, (8, N), 0)
    stores = []
    for j in range(CHUNKS):
        pltpu.make_async_copy(in4.at[j], in4.at[j], recv4.at[j]).wait()
        if j == 0:
            table_loads[1].wait()
        tiles = butterfly([in4[j, t] for t in range(SLOTS)], lane8)
        result = z_matmul(jnp.concatenate(tiles, axis=0), table_buf[1])
        stress_buf[2 * j : 2 * j + 2] = result.reshape(2, 16, 8, N)
        store = pltpu.make_async_copy(
            stress_buf.at[pl.ds(2 * j, 2)], stress_ref.at[pl.ds(2 * j, 2)], store_sem.at[j]
        )
        store.start()
        stores.append(store)
        for cell in range(CELLS):
            pick_z = jnp.broadcast_to(z_of[cell : cell + 1], (8, N))
            pick_row = jnp.broadcast_to(row_of[cell : cell + 1], (8, N))
            for c in range(2):
                total = jnp.zeros((8, N), F32)
                for t in range(4):
                    at = 128 * c + 32 * cell + 8 * t
                    tile = jnp.take_along_axis(result[at : at + 8], pick_z, axis=1, mode="promise_in_bounds")
                    total = total + jnp.where(pick_row == sublane + 8 * t, tile, 0.0)
                samp[HALO + cell, 2 * j + c : 2 * j + c + 1, :] = jnp.sum(total, axis=0, keepdims=True)

    samp_left = pltpu.make_async_remote_copy(
        src_ref=samp.at[pl.ds(HALO, 2)], dst_ref=samp.at[pl.ds(HALO + CELLS, 2)],
        send_sem=samp_send.at[0], recv_sem=samp_recv.at[0], device_id=left, device_id_type=MESH,
    )
    samp_right = pltpu.make_async_remote_copy(
        src_ref=samp.at[pl.ds(HALO + 2, 2)], dst_ref=samp.at[pl.ds(1, 2)],
        send_sem=samp_send.at[1], recv_sem=samp_recv.at[1], device_id=right, device_id_type=MESH,
    )
    samp_left.start()
    samp_right.start()
    samp_left.wait()
    samp_right.wait()

    sampled = [samp[:, c, :] for c in range(6)]

    def step(position, field):
        sigma = [sampled[c] + field[c] for c in range(6)]
        pull = [
            sum(sigma[full_index[a][b]] * burg[b] for b in range(3))
            for a in range(3)
        ]
        force = [
            pull[1] * line[2] - pull[2] * line[1],
            pull[2] * line[0] - pull[0] * line[2],
            pull[0] * line[1] - pull[1] * line[0],
        ]
        return [position[k] + step_size * force[k] for k in range(3)]

    position = step(start, field)
    for repeat in range(1, 3):
        field = pair_field(position, 1 + repeat, WIDE - 1 - repeat)
        position = step(position, field)
    for k in range(3):
        moved_ref[k, 0] = position[k][HALO : HALO + CELLS] - start[k][HALO : HALO + CELLS]

    for j in range(CHUNKS):
        pltpu.make_async_copy(out1.at[j, pl.ds(0, 31)], in1.at[j, pl.ds(0, 31)], send1.at[j]).wait()
        pltpu.make_async_copy(out2.at[j, pl.ds(0, 3)], in2.at[j, pl.ds(0, 3)], send2.at[j]).wait()
        pltpu.make_async_copy(out3.at[j, pl.ds(0, 3)], in3.at[j, pl.ds(0, 3)], send3.at[j]).wait()
        pltpu.make_async_copy(out4.at[j, pl.ds(0, 31)], in4.at[j, pl.ds(0, 31)], send4.at[j]).wait()
    for store in stores:
        store.wait()


def body(plastic, offsets, lines, burgers, counts, voxels):
    any_space = pl.BlockSpec(memory_space=pl.ANY)
    vmem = pl.BlockSpec(memory_space=pltpu.VMEM)
    dma = pltpu.SemaphoreType.DMA
    group = pltpu.VMEM((CHUNKS, SLOTS, 8, N), F32)
    along = pltpu.VMEM((CHUNKS, 4, 2, 32, N), F32)
    return pl.pallas_call(
        kernel,
        out_shape=(
            jax.ShapeDtypeStruct((6, 16, 8, N), F32),
            jax.ShapeDtypeStruct((3, 1, CELLS, N), F32),
        ),
        in_specs=[any_space, any_space, vmem, vmem, vmem, vmem, vmem],
        out_specs=(any_space, vmem),
        scratch_shapes=[
            pltpu.VMEM((6, 16, 8, N), F32),
            pltpu.VMEM((8, 2 * N, 2 * N), BF16),
            group, group, along, along,
            pltpu.VMEM((6, 2, 32, 2 * N), F32),
            along, along, group, group,
            pltpu.VMEM((6, 16, 8, N), F32),
            pltpu.VMEM((WIDE, 16, N), F32),
            pltpu.VMEM((WIDE, 8, N), F32),
            pltpu.VMEM((WIDE, 16, N), F32),
            pltpu.VMEM((3, WIDE, 16, N), F32),
            pltpu.VMEM((WIDE, 32, N), F32),
            dma((CHUNKS + 8,)),
            dma((CHUNKS,)), dma((CHUNKS,)), dma((CHUNKS,)), dma((CHUNKS,)),
            dma((CHUNKS,)), dma((CHUNKS,)), dma((CHUNKS,)), dma((CHUNKS,)),
            dma((2,)), dma((2,)), dma((2,)), dma((2,)), dma((CHUNKS,)),
        ],
        compiler_params=pltpu.CompilerParams(collective_id=0, has_side_effects=True),
    )(plastic, jnp.asarray(tables()), offsets, lines, burgers, counts, voxels)


def solution(mesh):
    placed = (
        P(None, "gx", "pa", None),
        P(None, "pa", "gx", None),
        P(None, "pa", "gx", None),
        P(None, "pa", "gx", None),
        P("pa", "gx"),
        P("pa", "gx", None),
    )
    return jax.shard_map(
        body,
        mesh=mesh,
        in_specs=placed,
        out_specs=(P(None, "gx", "pa", None), P(None, "pa", "gx", None)),
        check_vma=False,
    )
```

profile of v0, /device:TPU:1, one launch (start us, length us, event | category | flops | bytes accessed | tf_op | source)
XLA Modules:
  0.0 46.8 jit_solution(9833186478947363048)
XLA Ops:
  0.6 43.8 %shard_map.86 = (f32[6,16,8,128]{3,2,1,0:T(8,128)}, f32[3,1,4,128]{3,2,1,0:T(4,128)}) custom-call(f32[6,16,8,128]{3,2,1,0:T(8,128)} %plastic_ref.1, bf16[8,256,256]{2,1,0:T(8,128)(2,1)} %constant.2.clone.table_hbm, f32[3,1,4,128]{3,2,1,0:T(4,128)} %offsets_ref.1, f32[3,1,4,128]{3,2,1,0:T(4,128)} %lines_ref.1, f32[3,1,4,128]{3,2,1,0:T(4,128)} %burgers_ref.1, ...), custom_call_target="tpu_custom_call" | custom-call | tf_op jit(solution)/shard_map/pallas_call | solution.py:500
  44.4 0.0 copy-start
  44.4 1.8 %copy.11 = f32[6,16,8,128]{3,2,1,0:T(8,128)} copy(f32[6,16,8,128]{3,2,1,0:T(8,128)} %get-tuple-element.4) | data formatting | bytes 786432
  46.2 0.0 copy-done
  46.2 0.6 %copy.12 = f32[3,1,4,128]{3,2,1,0:T(4,128)} copy(f32[3,1,4,128]{3,2,1,0:T(4,128)S(1)} %copy-done) | data formatting | bytes 12288
Async XLA Ops:
  44.4 1.8 %copy-start = (f32[3,1,4,128]{3,2,1,0:T(4,128)S(1)}, f32[3,1,4,128]{3,2,1,0:T(4,128)}, u32[]{:S(2)}) copy-start(f32[3,1,4,128]{3,2,1,0:T(4,128)} %get-tuple-element.5) | copy-start | bytes 18436
where the time goes:
time: 47 us; the launch traced here: 46.8 us
  Pallas kernels  43.8 us (93%)
  local copies, waits for them, and re-layouts  2.37 us (5%)
  between operations  0.65 us (1%)
    pallas_call x1, Pallas kernels, body(): pl.pallas_call(kernel, out_shape=(jax.ShapeDtypeStruct((6, 16, 8, N), F32...  43.8 us
    unnamed x4, local copies, waits for them, and re-layouts  2.37 us

commit v1 on v0

v1 whole, which is shorter than its diff:
```python
import math

import jax
import jax.numpy as jnp
import numpy as np
from jax import lax
from jax.experimental import pallas as pl
from jax.experimental.pallas import tpu as pltpu
from jax.sharding import PartitionSpec as P

MESH = pl.DeviceIdType.MESH
F32 = jnp.float32
BF16 = jnp.bfloat16
N = 128
GX = 8
PA = 16
CHUNKS = ((0, 1, 2, 5, 3, 4),)
PAIRS = ((0, 1), (2, 5), (3, 4))
CELLS = 4
HALO = 3
WIDE = CELLS + 2 * HALO

lame_lambda = 1.5
shear_modulus = 1.0
green_coef = 2.5 / 3.5
core_square = 0.09
pair_factor = 1.0 / (4.0 * math.pi)
step_size = 0.05
full_index = ((0, 5, 4), (5, 1, 3), (4, 3, 2))


def np_split(table):
    table = np.asarray(table, np.float32)
    high = table.astype(jnp.bfloat16)
    low = (table - high.astype(np.float32)).astype(jnp.bfloat16)
    return high, low


def tables():
    index = np.arange(N)
    angle = 2.0 * np.pi * (np.outer(index, index) % N) / N
    cos, sin = np.cos(angle), np.sin(angle)
    flip = np.where(index % 2 == 0, 1.0, -1.0)
    bins, parity = index // 2, index % 2
    weight = np.where(bins == 0, 1.0, 2.0)[:, None] / N
    ahead_z = []
    for odd in range(2):
        imaginary = (parity == 1 - odd)[:, None]
        table = np.where(imaginary, -sin[bins], cos[bins])
        ahead_z.append(np.where(imaginary & (bins == 0)[:, None], flip[None, :], table))
    back_z = [table * weight for table in ahead_z]
    ky = np.arange(N // 2)
    ahead_y = np.concatenate([cos[:, ky], -sin[:, ky]], axis=1)
    ahead_y[:, N // 2] = flip
    back_y = ahead_y.T * np.where(index % 64 == 0, 1.0, 2.0)[:, None] / N
    plane = (index % 8) * 16 + index // 8
    cx, sx = cos[:, plane], sin[:, plane]
    ahead_x = [np.concatenate([cx, sx], axis=1), np.concatenate([sx, -cx], axis=1)]
    back_x = [np.concatenate([cx.T, -sx.T], axis=1) / N, np.concatenate([sx.T, cx.T], axis=1) / N]

    def beside(table):
        high, low = np_split(table)
        return np.block([[high, high], [low, np.zeros_like(low)]])

    def under(table):
        high, low = np_split(table)
        return np.block([[high, low], [high, np.zeros_like(low)]])

    def stacked(table):
        return np.concatenate(np_split(table), axis=0)

    out = [beside(ahead_z[0]), beside(ahead_z[1]), under(ahead_y)]
    out += [stacked(ahead_x[0]), stacked(ahead_x[1]), stacked(back_x[0]), stacked(back_x[1])]
    out += [under(back_y), beside(back_z[0].T), beside(back_z[1].T)]
    return np.stack(out), np.stack(back_z).astype(np.float32)


def split(value):
    high = value.astype(BF16)
    low = (value - high.astype(F32)).astype(BF16)
    return high, low


def dot(a, b, contract=(1, 0)):
    return lax.dot_general(a, b, (((contract[0],), (contract[1],)), ((), ())), preferred_element_type=F32)


def butterfly(value, lane):
    tiles = [value[8 * t : 8 * t + 8] for t in range(PA)]
    step = PA // 2
    while step >= 1:
        bit = (lane & (step * 8)) != 0
        for index in range(PA):
            if index & step == 0:
                first, second = tiles[index], tiles[index + step]
                tiles[index] = jnp.where(bit, pltpu.roll(second, step * 8, 1), first)
                tiles[index + step] = jnp.where(bit, second, pltpu.roll(first, N - step * 8, 1))
        step //= 2
    return jnp.concatenate(tiles, axis=0)


def turned(value, upper):
    other = pltpu.roll(value, N // 2, 1)
    return jnp.where(upper, -other, other)


def y_matmul(rows, table):
    high, low = split(rows)
    both = dot(jnp.concatenate([high, low], axis=1), table)
    return both[:, :N] + both[:, N:]


def x_matmul(table, first, second, upper):
    top = jnp.concatenate([first, second], axis=1)
    below = jnp.concatenate([turned(first, upper), turned(second, upper)], axis=1)
    high, low = split(jnp.concatenate([top, below], axis=0))
    both = dot(table, high)
    result = both[:N] + both[N:] + dot(table[:N], low)
    return result[:, :N], result[:, N:]


def stress_terms(strain, freq_x, freq_y, freq_z):
    xx, yy, zz, yz, xz, xy = strain
    trace = xx + yy + zz
    tau_xx = lame_lambda * trace + 2.0 * shear_modulus * xx
    tau_yy = lame_lambda * trace + 2.0 * shear_modulus * yy
    tau_zz = lame_lambda * trace + 2.0 * shear_modulus * zz
    tau_yz = 2.0 * shear_modulus * yz
    tau_xz = 2.0 * shear_modulus * xz
    tau_xy = 2.0 * shear_modulus * xy
    norm_x = tau_xx * freq_x + tau_xy * freq_y + tau_xz * freq_z
    norm_y = tau_xy * freq_x + tau_yy * freq_y + tau_yz * freq_z
    norm_z = tau_xz * freq_x + tau_yz * freq_y + tau_zz * freq_z
    square = freq_x * freq_x + freq_y * freq_y + freq_z * freq_z
    inverse = 1.0 / jnp.maximum(square, 1.0)
    along = (freq_x * norm_x + freq_y * norm_y + freq_z * norm_z) * inverse * inverse * green_coef
    half = inverse / (2.0 * shear_modulus)

    def term(first_q, second_q, first_n, second_n, plastic):
        total = (first_q * second_n + second_q * first_n) * half - first_q * second_q * along
        return total - plastic

    el_xx = term(freq_x, freq_x, norm_x, norm_x, xx)
    el_yy = term(freq_y, freq_y, norm_y, norm_y, yy)
    el_zz = term(freq_z, freq_z, norm_z, norm_z, zz)
    el_yz = term(freq_y, freq_z, norm_y, norm_z, yz)
    el_xz = term(freq_x, freq_z, norm_x, norm_z, xz)
    el_xy = term(freq_x, freq_y, norm_x, norm_y, xy)
    el_trace = el_xx + el_yy + el_zz
    return (
        lame_lambda * el_trace + 2.0 * shear_modulus * el_xx,
        lame_lambda * el_trace + 2.0 * shear_modulus * el_yy,
        lame_lambda * el_trace + 2.0 * shear_modulus * el_zz,
        2.0 * shear_modulus * el_yz,
        2.0 * shear_modulus * el_xz,
        2.0 * shear_modulus * el_xy,
    )


def signed_frequency(index):
    value = jnp.where(index < N // 2, index, jnp.where(index == N // 2, 0, index - N))
    return value.astype(F32)


def kernel(
    plastic_hbm, table_hbm, back_hbm, offsets_hbm, lines_hbm, burgers_hbm, counts_hbm, voxels_hbm,
    stress_hbm, moved_hbm,
    plastic_buf, table_buf, back_buf, offsets_ref, lines_ref, burgers_ref, counts_ref, voxels_ref, moved_ref,
    out1, in1, out2, in2, spec, stress_buf, seg, samp, lbuf, mbuf, pair_out,
    load_sem, send1, recv1, send2, recv2, halo_send, halo_recv, samp_send, samp_recv, store_sem,
):
    gx = lax.axis_index("gx")
    pa = lax.axis_index("pa")
    mode = pa * GX + gx
    left = {"gx": (gx + 7) % 8}
    right = {"gx": (gx + 1) % 8}
    place = {c: (j, row) for j, chunk in enumerate(CHUNKS) for row, c in enumerate(chunk)}

    def device(i):
        return {"gx": gx ^ (i & 7), "pa": pa ^ (i >> 3)}

    sources = (plastic_hbm, offsets_hbm, lines_hbm, burgers_hbm, counts_hbm, voxels_hbm, back_hbm)
    targets = (plastic_buf, offsets_ref, lines_ref, burgers_ref, counts_ref, voxels_ref, back_buf)
    loads = [
        pltpu.make_async_copy(source, target, load_sem.at[i])
        for i, (source, target) in enumerate(zip(sources, targets))
    ]
    table_loads = [
        pltpu.make_async_copy(table_hbm.at[i], table_buf.at[i], load_sem.at[len(loads) + i]) for i in range(10)
    ]
    barrier = pltpu.get_barrier_semaphore()
    with jax.named_scope("greet"):
        loads[0].start()
        table_loads[0].start()
        table_loads[1].start()
        for i in range(N - 1, 0, -1):
            pl.semaphore_signal(barrier, inc=1, device_id=device(i), device_id_type=MESH)
        for copy in loads[1:] + table_loads[2:]:
            copy.start()

    lane8 = lax.broadcasted_iota(jnp.int32, (8, N), 1)
    upper = lax.broadcasted_iota(jnp.int32, (N, N), 1) >= N // 2

    def send_all(j, source, target, send_sem, recv_sem):
        rows = pl.ds(0, len(CHUNKS[j]))
        for i in range(N - 1, 0, -1):
            pltpu.make_async_remote_copy(
                src_ref=source.at[j, mode ^ i, rows], dst_ref=target.at[j, mode, rows],
                send_sem=send_sem.at[j], recv_sem=recv_sem.at[j],
                device_id=device(i), device_id_type=MESH,
            ).start()
        pltpu.make_async_copy(source.at[j, mode, rows], target.at[j, mode, rows], recv_sem.at[j]).start()

    def wait_all(j, target, recv_sem):
        whole = target.at[j, :, pl.ds(0, len(CHUNKS[j]))]
        pltpu.make_async_copy(whole, whole, recv_sem.at[j]).wait()

    def put(target, c, value):
        j, row = place[c]
        target.reshape(len(CHUNKS) * N * 8, N)[pl.ds(j * N * 8 + row, N, stride=8), :] = value

    def take(source, c):
        j, row = place[c]
        return source.reshape(len(CHUNKS) * N * 8, N)[pl.ds(j * N * 8 + row, N, stride=8), :]

    with jax.named_scope("wait_load"):
        loads[0].wait()
        table_loads[0].wait()
        table_loads[1].wait()
    with jax.named_scope("z_ahead"):
        for pair in PAIRS:
            rows = jnp.concatenate([plastic_buf[c].reshape(N, N) for c in pair], axis=0)
            high, low = split(rows)
            both = dot(table_buf[1 if pair[0] == 3 else 0], jnp.concatenate([high, low], axis=1), (1, 1))
            result = both[:N] + both[N:]
            put(out1, pair[0], result[:, :N])
            put(out1, pair[1], result[:, N:])
    with jax.named_scope("wait_barrier"):
        pl.semaphore_wait(barrier, N - 1)
    with jax.named_scope("send1"):
        for j in range(len(CHUNKS)):
            send_all(j, out1, in1, send1, recv1)

    for copy in loads[1:6]:
        copy.wait()
    counts = counts_ref[...]
    index = lax.broadcasted_iota(jnp.int32, (CELLS, N), 1)
    live = (index < counts.reshape(CELLS, 1)).astype(F32)
    first_position = []
    for k in range(3):
        value = offsets_ref[k, 0] - 0.5
        seg[HALO : HALO + CELLS, k, :] = value
        seg[HALO : HALO + CELLS, 3 + k, :] = lines_ref[k, 0]
        seg[HALO : HALO + CELLS, 6 + k, :] = burgers_ref[k, 0] * live
    to_left = pltpu.make_async_remote_copy(
        src_ref=seg.at[pl.ds(HALO, HALO)], dst_ref=seg.at[pl.ds(HALO + CELLS, HALO)],
        send_sem=halo_send.at[0], recv_sem=halo_recv.at[0], device_id=left, device_id_type=MESH,
    )
    to_right = pltpu.make_async_remote_copy(
        src_ref=seg.at[pl.ds(CELLS, HALO)], dst_ref=seg.at[pl.ds(0, HALO)],
        send_sem=halo_send.at[1], recv_sem=halo_recv.at[1], device_id=right, device_id_type=MESH,
    )
    to_left.start()
    to_right.start()

    for copy in table_loads[2:]:
        copy.wait()
    loads[6].wait()
    for j in range(len(CHUNKS)):
        with jax.named_scope("wait_in1"):
            wait_all(j, in1, recv1)
        with jax.named_scope("y_ahead"):
            for c in CHUNKS[j]:
                spec[c] = y_matmul(butterfly(take(in1, c), lane8), table_buf[2])
    with jax.named_scope("x_ahead"):
        for pair in PAIRS:
            table = table_buf[4 if pair[0] == 3 else 3]
            spec[pair[0]], spec[pair[1]] = x_matmul(table, spec[pair[0]], spec[pair[1]], upper)

    with jax.named_scope("operator"):
        freq_y = signed_frequency(lane8 % 64)
        freq_z = jnp.where(mode % 2 == 0, mode // 2, -(mode // 2)).astype(F32)
        for t in range(N // 8):
            freq_x = signed_frequency(lax.broadcasted_iota(jnp.int32, (8, N), 0) + 8 * t)
            strain = [spec[c, 8 * t : 8 * t + 8, :] for c in range(6)]
            result = stress_terms(strain, freq_x, freq_y, freq_z)
            for c in range(6):
                spec[c, 8 * t : 8 * t + 8, :] = result[c]

    with jax.named_scope("x_back"):
        for pair in PAIRS:
            table = table_buf[6 if pair[0] == 3 else 5]
            spec[pair[0]], spec[pair[1]] = x_matmul(table, spec[pair[0]], spec[pair[1]], upper)
    for j in range(len(CHUNKS)):
        with jax.named_scope("y_back"):
            for c in CHUNKS[j]:
                put(out2, c, butterfly(y_matmul(spec[c], table_buf[7]), lane8))
        with jax.named_scope("send2"):
            send_all(j, out2, in2, send2, recv2)

    with jax.named_scope("wait_halo"):
        to_left.wait()
        to_right.wait()
    line = [seg[:, 3 + k, :] for k in range(3)]
    burg = [seg[:, 6 + k, :] for k in range(3)]
    start = [seg[:, k, :] for k in range(3)]
    lbuf[...] = jnp.zeros_like(lbuf)
    mbuf[...] = jnp.zeros_like(mbuf)
    for c in range(3):
        for b in range(3):
            lbuf[:, 3 * c + b, :] = line[c] * burg[b]

    def pair_field(position, low, high):
        arm = [
            position[1] * line[2] - position[2] * line[1],
            position[2] * line[0] - position[0] * line[2],
            position[0] * line[1] - position[1] * line[0],
        ]
        for shift in range(3):
            moved_arm = [
                arm[0],
                arm[1] - (shift - 1.0) * line[2],
                arm[2] + (shift - 1.0) * line[1],
            ]
            for a in range(3):
                for b in range(3):
                    mbuf[shift, :, 3 * a + b, :] = moved_arm[a] * burg[b]
        pad = jnp.zeros((16 - WIDE, N), F32)
        columns = [jnp.transpose(jnp.concatenate([value, pad], axis=0)) for value in position]
        for cell in range(low, high):
            target = [value[cell : cell + 1] for value in position]
            weights, factors = [], []
            for shift in range(3):
                source = cell + shift - 1
                delta = [
                    target[k] - (shift - 1.0) * (k == 0) - columns[k][:, source : source + 1] for k in range(3)
                ]
                radius = delta[0] * delta[0] + delta[1] * delta[1] + delta[2] * delta[2] + core_square
                root = lax.rsqrt(radius)
                weights.append(root * root * root)
                factors.append(jnp.concatenate([lbuf[source], mbuf[shift, source]], axis=0))
            weight_high, weight_low = split(jnp.concatenate(weights, axis=0))
            factor_high, factor_low = split(jnp.concatenate(factors, axis=1))
            both = dot(jnp.concatenate([factor_high, factor_low], axis=0), weight_high)
            pair_out[cell] = both[:32] + both[32:] + dot(factor_high, weight_low)
        spread = [[pair_out[:, 3 * c + b, :] for b in range(3)] for c in range(3)]
        offset = [[pair_out[:, 16 + 3 * a + b, :] for b in range(3)] for a in range(3)]
        moment = [[None] * 3 for _ in range(3)]
        for b in range(3):
            for a in range(3):
                n, m = (a + 1) % 3, (a + 2) % 3
                moment[a][b] = position[n] * spread[m][b] - position[m] * spread[n][b] - offset[a][b]
        return [
            pair_factor * (moment[a][b] + moment[b][a])
            for a, b in ((0, 0), (1, 1), (2, 2), (1, 2), (0, 2), (0, 1))
        ]

    pair_out[...] = jnp.zeros_like(pair_out)
    with jax.named_scope("pair1"):
        field = pair_field(start, 1, WIDE - 1)

    voxels = voxels_ref[0]
    column_of = voxels >> 7
    z_of = voxels & 127
    for j in range(len(CHUNKS)):
        with jax.named_scope("wait_in2"):
            wait_all(j, in2, recv2)
    with jax.named_scope("sample"):
        for c in range(6):
            stress_buf[c] = take(in2, c)
        for cell in range(CELLS):
            pick_z = jnp.broadcast_to(z_of[cell : cell + 1], (8, N))
            pick = jnp.broadcast_to(column_of[cell : cell + 1], (8, N))
            total = [None] * 6
            for t in range(N // 8):
                rows = slice(8 * t, 8 * t + 8)
                factor = [
                    jnp.take_along_axis(back_buf[odd, rows], pick_z, axis=1, mode="promise_in_bounds")
                    for odd in range(2)
                ]
                for c in range(6):
                    tile = jnp.take_along_axis(stress_buf[c, rows], pick, axis=1, mode="promise_in_bounds")
                    term = tile * factor[1 if c in (3, 4) else 0]
                    total[c] = term if t == 0 else total[c] + term
            for c in range(6):
                samp[HALO + cell, c : c + 1, :] = jnp.sum(total[c], axis=0, keepdims=True)

    samp_left = pltpu.make_async_remote_copy(
        src_ref=samp.at[pl.ds(HALO, 2)], dst_ref=samp.at[pl.ds(HALO + CELLS, 2)],
        send_sem=samp_send.at[0], recv_sem=samp_recv.at[0], device_id=left, device_id_type=MESH,
    )
    samp_right = pltpu.make_async_remote_copy(
        src_ref=samp.at[pl.ds(HALO + 2, 2)], dst_ref=samp.at[pl.ds(1, 2)],
        send_sem=samp_send.at[1], recv_sem=samp_recv.at[1], device_id=right, device_id_type=MESH,
    )
    samp_left.start()
    samp_right.start()
    stores = []
    with jax.named_scope("z_back"):
        for pair in PAIRS:
            table = table_buf[9 if pair[0] == 3 else 8]
            high, low = split(jnp.concatenate([stress_buf[c] for c in pair], axis=1))
            both = dot(table, jnp.concatenate([high, low], axis=0))
            result = both[:N] + both[N:]
            for c, half in zip(pair, (result[:, :N], result[:, N:])):
                plastic_buf[c] = jnp.transpose(half).reshape(16, 8, N)
                store = pltpu.make_async_copy(plastic_buf.at[c], stress_hbm.at[c], store_sem.at[c])
                store.start()
                stores.append(store)
    with jax.named_scope("wait_samp"):
        samp_left.wait()
        samp_right.wait()

    sampled = [samp[:, c, :] for c in range(6)]

    def step(position, field):
        sigma = [sampled[c] + field[c] for c in range(6)]
        pull = [
            sum(sigma[full_index[a][b]] * burg[b] for b in range(3))
            for a in range(3)
        ]
        force = [
            pull[1] * line[2] - pull[2] * line[1],
            pull[2] * line[0] - pull[0] * line[2],
            pull[0] * line[1] - pull[1] * line[0],
        ]
        return [position[k] + step_size * force[k] for k in range(3)]

    position = step(start, field)
    for repeat in range(1, 3):
        with jax.named_scope("pair_later"):
            field = pair_field(position, 1 + repeat, WIDE - 1 - repeat)
        position = step(position, field)
    for k in range(3):
        moved_ref[k, 0] = position[k][HALO : HALO + CELLS] - start[k][HALO : HALO + CELLS]
    moved_store = pltpu.make_async_copy(moved_ref, moved_hbm, store_sem.at[6])
    moved_store.start()
    stores.append(moved_store)

    with jax.named_scope("drain_mark"):
        stores[0].wait()
    for j in range(len(CHUNKS)):
        for source, send_sem in ((out1, send1), (out2, send2)):
            sent = source.at[j, pl.ds(0, N - 1), pl.ds(0, len(CHUNKS[j]))]
            pltpu.make_async_copy(sent, sent, send_sem.at[j]).wait()
    for store in stores[1:]:
        store.wait()


def body(plastic, offsets, lines, burgers, counts, voxels):
    any_space = pl.BlockSpec(memory_space=pl.ANY)
    dma = pltpu.SemaphoreType.DMA
    group = pltpu.VMEM((len(CHUNKS), N, 8, N), F32)
    vectors = pltpu.VMEM((3, 1, CELLS, N), F32)
    table, back = tables()
    return pl.pallas_call(
        kernel,
        out_shape=(
            jax.ShapeDtypeStruct((6, 16, 8, N), F32),
            jax.ShapeDtypeStruct((3, 1, CELLS, N), F32),
        ),
        in_specs=[any_space] * 8,
        out_specs=(any_space, any_space),
        scratch_shapes=[
            pltpu.VMEM((6, 16, 8, N), F32),
            pltpu.VMEM((10, 2 * N, 2 * N), BF16),
            pltpu.VMEM((2, N, N), F32),
            vectors, vectors, vectors,
            pltpu.VMEM((1, CELLS), jnp.int32),
            pltpu.VMEM((1, CELLS, N), jnp.int32),
            vectors,
            group, group, group, group,
            pltpu.VMEM((6, N, N), F32),
            pltpu.VMEM((6, N, N), F32),
            pltpu.VMEM((WIDE, 16, N), F32),
            pltpu.VMEM((WIDE, 8, N), F32),
            pltpu.VMEM((WIDE, 16, N), F32),
            pltpu.VMEM((3, WIDE, 16, N), F32),
            pltpu.VMEM((WIDE, 32, N), F32),
            dma((17,)),
            dma((len(CHUNKS),)), dma((len(CHUNKS),)), dma((len(CHUNKS),)), dma((len(CHUNKS),)),
            dma((2,)), dma((2,)), dma((2,)), dma((2,)), dma((7,)),
        ],
        compiler_params=pltpu.CompilerParams(collective_id=0, has_side_effects=True),
    )(plastic, jnp.asarray(table), jnp.asarray(back), offsets, lines, burgers, counts, voxels)


def solution(mesh):
    placed = (
        P(None, "gx", "pa", None),
        P(None, "pa", "gx", None),
        P(None, "pa", "gx", None),
        P(None, "pa", "gx", None),
        P("pa", "gx"),
        P("pa", "gx", None),
    )
    return jax.shard_map(
        body,
        mesh=mesh,
        in_specs=placed,
        out_specs=(P(None, "gx", "pa", None), P(None, "pa", "gx", None)),
        check_vma=False,
    )
```

time: 47 us -> 38.6 us (0.82)
  Pallas kernels: 43.8 us -> 34.4 us
  local copies, waits for them, and re-layouts: 2.37 us -> 3.05 us
    pallas_call x1, Pallas kernels: 43.8 us -> 34.4 us  [body(): pl.pallas_call(kernel, out_shape=(jax.ShapeDtypeStruct((6, 16, 8, N), F32...]
    unnamed x4 -> x2, local copies, waits for them, and re-layouts: 2.37 us -> 3.05 us
where the time goes in v1:
time: 38.6 us; the launch traced here: 38.1 us
  Pallas kernels  34.4 us (89%)
  local copies, waits for them, and re-layouts  3.05 us (8%)
  between operations  0.64 us (2%)
    pallas_call x1, Pallas kernels, body(): pl.pallas_call(kernel, out_shape=(jax.ShapeDtypeStruct((6, 16, 8, N), F32...  34.4 us
    unnamed x2, local copies, waits for them, and re-layouts  3.05 us

profile of v1, /device:TPU:1, one launch (start us, length us, event | category | flops | bytes accessed | tf_op | source)
XLA Modules:
  0.0 38.1 jit_solution(15126013905545846650)
XLA Ops:
  0.6 34.4 %shard_map.95 = (f32[6,16,8,128]{3,2,1,0:T(8,128)}, f32[3,1,4,128]{3,2,1,0:T(4,128)}) custom-call(f32[6,16,8,128]{3,2,1,0:T(8,128)} %plastic_hbm.1, bf16[10,256,256]{2,1,0:T(8,128)(2,1)} %constant.4.clone.table_hbm, f32[2,128,128]{2,1,0:T(8,128)} %constant.5.clone.back_hbm, f32[3,1,4,128]{3,2,1,0:T(4,128)} %offsets_hbm.1, f32[3,1,4,128]{3,2,1,0:T(4,128)} %lines_hbm.1, ...), custom_call_target="tpu_custom_call" | custom-call | tf_op jit(solution)/shard_map/pallas_call | solution.py:456
  35.0 1.8 %copy.12 = f32[6,16,8,128]{3,2,1,0:T(8,128)} copy(f32[6,16,8,128]{3,2,1,0:T(8,128)} %get-tuple-element.4) | data formatting | bytes 786432
  36.8 1.3 %copy.13 = f32[3,1,4,128]{3,2,1,0:T(4,128)} copy(f32[3,1,4,128]{3,2,1,0:T(4,128)} %get-tuple-element.5) | data formatting | bytes 12288

commit v2 on v1

--- a/solution.py
+++ b/solution.py
@@ -19,6 +19,10 @@
 CELLS = 4
 HALO = 3
 WIDE = CELLS + 2 * HALO
+OWN_SECOND = ((3, (1, 2), True), (4, (0, 1, 2), True), (5, (0, 1, 2), True), (6, (0, 1), True))
+REST_SECOND = ((2, (0, 1, 2), True), (3, (0,), False), (6, (2,), False), (7, (0, 1, 2), True))
+OWN_THIRD = ((4, (1, 2), True), (5, (0, 1), True))
+REST_THIRD = ((3, (0, 1, 2), True), (4, (0,), False), (5, (2,), False), (6, (0, 1, 2), True))
 
 lame_lambda = 1.5
 shear_modulus = 1.0
@@ -157,17 +161,91 @@
     )
 
 
+def partners():
+    hops = (0, 1, 2, 1)
+
+    def distance(i):
+        low, high = i & 7, i >> 3
+        return hops[2 * (high >> 3) + (low & 1)] + hops[low >> 1] + hops[(high >> 1) & 3]
+
+    return sorted(range(1, N), key=lambda i: -distance(i))
+
+
 def signed_frequency(index):
     value = jnp.where(index < N // 2, index, jnp.where(index == N // 2, 0, index - N))
     return value.astype(F32)
 
 
+def arms_into(mbuf, position, line, burg):
+    arm = [
+        position[1] * line[2] - position[2] * line[1],
+        position[2] * line[0] - position[0] * line[2],
+        position[0] * line[1] - position[1] * line[0],
+    ]
+    for shift in range(3):
+        moved_arm = [
+            arm[0],
+            arm[1] - (shift - 1.0) * line[2],
+            arm[2] + (shift - 1.0) * line[1],
+        ]
+        for a in range(3):
+            for b in range(3):
+                mbuf[shift, :, 3 * a + b, :] = moved_arm[a] * burg[b]
+
+
+def pair_blocks(position, lbuf, mbuf, pair_out, blocks):
+    pad = jnp.zeros((16 - WIDE, N), F32)
+    columns = [jnp.transpose(jnp.concatenate([value, pad], axis=0)) for value in position]
+    for cell, shifts, fresh in blocks:
+        target = [value[cell : cell + 1] for value in position]
+        weights, factors = [], []
+        for shift in shifts:
+            source = cell + shift - 1
+            delta = [
+                (target[k] - (shift - 1.0) * (k == 0)) - columns[k][:, source : source + 1] for k in range(3)
+            ]
+            radius = delta[0] * delta[0] + delta[1] * delta[1] + delta[2] * delta[2] + core_square
+            root = lax.rsqrt(radius)
+            weights.append(root * root * root)
+            factors.append(jnp.concatenate([lbuf[source], mbuf[shift, source]], axis=0))
+        weight_high, weight_low = split(jnp.concatenate(weights, axis=0))
+        factor_high, factor_low = split(jnp.concatenate(factors, axis=1))
+        both = dot(jnp.concatenate([factor_high, factor_low], axis=0), weight_high)
+        total = both[:32] + both[32:] + dot(factor_high, weight_low)
+        pair_out[cell] = total if fresh else pair_out[cell] + total
+
+
+def pair_field(position, pair_out):
+    spread = [[pair_out[:, 3 * c + b, :] for b in range(3)] for c in range(3)]
+    offset = [[pair_out[:, 16 + 3 * a + b, :] for b in range(3)] for a in range(3)]
+    moment = [[None] * 3 for _ in range(3)]
+    for b in range(3):
+        for a in range(3):
+            n, m = (a + 1) % 3, (a + 2) % 3
+            moment[a][b] = position[n] * spread[m][b] - position[m] * spread[n][b] - offset[a][b]
+    return [
+        pair_factor * (moment[a][b] + moment[b][a])
+        for a, b in ((0, 0), (1, 1), (2, 2), (1, 2), (0, 2), (0, 1))
+    ]
+
+
+def advance(position, sampled, field, line, burg):
+    sigma = [sampled[c] + field[c] for c in range(6)]
+    pull = [sum(sigma[full_index[a][b]] * burg[b] for b in range(3)) for a in range(3)]
+    force = [
+        pull[1] * line[2] - pull[2] * line[1],
+        pull[2] * line[0] - pull[0] * line[2],
+        pull[0] * line[1] - pull[1] * line[0],
+    ]
+    return [position[k] + step_size * force[k] for k in range(3)]
+
+
 def kernel(
     plastic_hbm, table_hbm, back_hbm, offsets_hbm, lines_hbm, burgers_hbm, counts_hbm, voxels_hbm,
-    stress_hbm, moved_hbm,
-    plastic_buf, table_buf, back_buf, offsets_ref, lines_ref, burgers_ref, counts_ref, voxels_ref, moved_ref,
-    out1, in1, out2, in2, spec, stress_buf, seg, samp, lbuf, mbuf, pair_out,
-    load_sem, send1, recv1, send2, recv2, halo_send, halo_recv, samp_send, samp_recv, store_sem,
+    stress_out, seg_out, samp_out, field_out, lbuf, second_out, third_out,
+    plastic_buf, table_buf, back_buf, offsets_ref, lines_ref, burgers_ref, counts_ref, voxels_ref,
+    out1, in1, out2, in2, spec, stress_buf, seg, samp, own, mbuf, pair_out, factor_buf,
+    load_sem, send1, recv1, send2, recv2, halo_send, halo_recv, samp_send, samp_recv,
 ):
     gx = lax.axis_index("gx")
     pa = lax.axis_index("pa")
@@ -193,7 +271,7 @@
         loads[0].start()
         table_loads[0].start()
         table_loads[1].start()
-        for i in range(N - 1, 0, -1):
+        for i in partners():
             pl.semaphore_signal(barrier, inc=1, device_id=device(i), device_id_type=MESH)
         for copy in loads[1:] + table_loads[2:]:
             copy.start()
@@ -203,7 +281,7 @@
 
     def send_all(j, source, target, send_sem, recv_sem):
         rows = pl.ds(0, len(CHUNKS[j]))
-        for i in range(N - 1, 0, -1):
+        for i in partners():
             pltpu.make_async_remote_copy(
                 src_ref=source.at[j, mode ^ i, rows], dst_ref=target.at[j, mode, rows],
                 send_sem=send_sem.at[j], recv_sem=recv_sem.at[j],
@@ -304,64 +382,35 @@
     line = [seg[:, 3 + k, :] for k in range(3)]
     burg = [seg[:, 6 + k, :] for k in range(3)]
     start = [seg[:, k, :] for k in range(3)]
-    lbuf[...] = jnp.zeros_like(lbuf)
-    mbuf[...] = jnp.zeros_like(mbuf)
-    for c in range(3):
-        for b in range(3):
-            lbuf[:, 3 * c + b, :] = line[c] * burg[b]
-
-    def pair_field(position, low, high):
-        arm = [
-            position[1] * line[2] - position[2] * line[1],
-            position[2] * line[0] - position[0] * line[2],
-            position[0] * line[1] - position[1] * line[0],
-        ]
-        for shift in range(3):
-            moved_arm = [
-                arm[0],
-                arm[1] - (shift - 1.0) * line[2],
-                arm[2] + (shift - 1.0) * line[1],
-            ]
-            for a in range(3):
-                for b in range(3):
-                    mbuf[shift, :, 3 * a + b, :] = moved_arm[a] * burg[b]
-        pad = jnp.zeros((16 - WIDE, N), F32)
-        columns = [jnp.transpose(jnp.concatenate([value, pad], axis=0)) for value in position]
-        for cell in range(low, high):
-            target = [value[cell : cell + 1] for value in position]
-            weights, factors = [], []
-            for shift in range(3):
-                source = cell + shift - 1
-                delta = [
-                    target[k] - (shift - 1.0) * (k == 0) - columns[k][:, source : source + 1] for k in range(3)
-                ]
-                radius = delta[0] * delta[0] + delta[1] * delta[1] + delta[2] * delta[2] + core_square
-                root = lax.rsqrt(radius)
-                weights.append(root * root * root)
-                factors.append(jnp.concatenate([lbuf[source], mbuf[shift, source]], axis=0))
-            weight_high, weight_low = split(jnp.concatenate(weights, axis=0))
-            factor_high, factor_low = split(jnp.concatenate(factors, axis=1))
-            both = dot(jnp.concatenate([factor_high, factor_low], axis=0), weight_high)
-            pair_out[cell] = both[:32] + both[32:] + dot(factor_high, weight_low)
-        spread = [[pair_out[:, 3 * c + b, :] for b in range(3)] for c in range(3)]
-        offset = [[pair_out[:, 16 + 3 * a + b, :] for b in range(3)] for a in range(3)]
-        moment = [[None] * 3 for _ in range(3)]
-        for b in range(3):
-            for a in range(3):
-                n, m = (a + 1) % 3, (a + 2) % 3
-                moment[a][b] = position[n] * spread[m][b] - position[m] * spread[n][b] - offset[a][b]
-        return [
-            pair_factor * (moment[a][b] + moment[b][a])
-            for a, b in ((0, 0), (1, 1), (2, 2), (1, 2), (0, 2), (0, 1))
-        ]
-
-    pair_out[...] = jnp.zeros_like(pair_out)
+    seg_out[...] = seg[...]
     with jax.named_scope("pair1"):
-        field = pair_field(start, 1, WIDE - 1)
+        lbuf[...] = jnp.zeros_like(lbuf)
+        mbuf[...] = jnp.zeros_like(mbuf)
+        pair_out[...] = jnp.zeros_like(pair_out)
+        own[...] = jnp.zeros_like(own)
+        for c in range(3):
+            for b in range(3):
+                lbuf[:, 3 * c + b, :] = line[c] * burg[b]
+        arms_into(mbuf, start, line, burg)
+        pair_blocks(start, lbuf, mbuf, pair_out, [(cell, (0, 1, 2), True) for cell in range(1, WIDE - 1)])
+        field = pair_field(start, pair_out)
+        for c in range(6):
+            field_out[c] = field[c]
+        second_out[...] = jnp.zeros_like(second_out)
+        third_out[...] = jnp.zeros_like(third_out)
 
     voxels = voxels_ref[0]
     column_of = voxels >> 7
     z_of = voxels & 127
+    with jax.named_scope("factors"):
+        for cell in range(CELLS):
+            pick_z = jnp.broadcast_to(z_of[cell : cell + 1], (8, N))
+            for odd in range(2):
+                for t in range(N // 8):
+                    rows = slice(8 * t, 8 * t + 8)
+                    factor_buf[cell, odd, rows] = jnp.take_along_axis(
+                        back_buf[odd, rows], pick_z, axis=1, mode="promise_in_bounds"
+                    )
     for j in range(len(CHUNKS)):
         with jax.named_scope("wait_in2"):
             wait_all(j, in2, recv2)
@@ -369,21 +418,19 @@
         for c in range(6):
             stress_buf[c] = take(in2, c)
         for cell in range(CELLS):
-            pick_z = jnp.broadcast_to(z_of[cell : cell + 1], (8, N))
             pick = jnp.broadcast_to(column_of[cell : cell + 1], (8, N))
             total = [None] * 6
             for t in range(N // 8):
                 rows = slice(8 * t, 8 * t + 8)
-                factor = [
-                    jnp.take_along_axis(back_buf[odd, rows], pick_z, axis=1, mode="promise_in_bounds")
-                    for odd in range(2)
-                ]
+                factor = [factor_buf[cell, odd, rows] for odd in range(2)]
                 for c in range(6):
                     tile = jnp.take_along_axis(stress_buf[c, rows], pick, axis=1, mode="promise_in_bounds")
                     term = tile * factor[1 if c in (3, 4) else 0]
                     total[c] = term if t == 0 else total[c] + term
             for c in range(6):
-                samp[HALO + cell, c : c + 1, :] = jnp.sum(total[c], axis=0, keepdims=True)
+                value = jnp.sum(total[c], axis=0, keepdims=True)
+                samp[HALO + cell, c : c + 1, :] = value
+                own[HALO + cell, c : c + 1, :] = value
 
     samp_left = pltpu.make_async_remote_copy(
         src_ref=samp.at[pl.ds(HALO, 2)], dst_ref=samp.at[pl.ds(HALO + CELLS, 2)],
@@ -395,7 +442,6 @@
     )
     samp_left.start()
     samp_right.start()
-    stores = []
     with jax.named_scope("z_back"):
         for pair in PAIRS:
             table = table_buf[9 if pair[0] == 3 else 8]
@@ -403,48 +449,58 @@
             both = dot(table, jnp.concatenate([high, low], axis=0))
             result = both[:N] + both[N:]
             for c, half in zip(pair, (result[:, :N], result[:, N:])):
-                plastic_buf[c] = jnp.transpose(half).reshape(16, 8, N)
-                store = pltpu.make_async_copy(plastic_buf.at[c], stress_hbm.at[c], store_sem.at[c])
-                store.start()
-                stores.append(store)
+                stress_out[c] = jnp.transpose(half).reshape(16, 8, N)
+    with jax.named_scope("pair_own"):
+        position = advance(start, [own[:, c, :] for c in range(6)], field, line, burg)
+        arms_into(mbuf, position, line, burg)
+        pair_blocks(position, lbuf, mbuf, second_out, OWN_SECOND)
+        position = advance(
+            position, [own[:, c, :] for c in range(6)], pair_field(position, second_out), line, burg
+        )
+        arms_into(mbuf, position, line, burg)
+        pair_blocks(position, lbuf, mbuf, third_out, OWN_THIRD)
+
     with jax.named_scope("wait_samp"):
         samp_left.wait()
         samp_right.wait()
-
-    sampled = [samp[:, c, :] for c in range(6)]
-
-    def step(position, field):
-        sigma = [sampled[c] + field[c] for c in range(6)]
-        pull = [
-            sum(sigma[full_index[a][b]] * burg[b] for b in range(3))
-            for a in range(3)
-        ]
-        force = [
-            pull[1] * line[2] - pull[2] * line[1],
-            pull[2] * line[0] - pull[0] * line[2],
-            pull[0] * line[1] - pull[1] * line[0],
-        ]
-        return [position[k] + step_size * force[k] for k in range(3)]
-
-    position = step(start, field)
-    for repeat in range(1, 3):
-        with jax.named_scope("pair_later"):
-            field = pair_field(position, 1 + repeat, WIDE - 1 - repeat)
-        position = step(position, field)
-    for k in range(3):
-        moved_ref[k, 0] = position[k][HALO : HALO + CELLS] - start[k][HALO : HALO + CELLS]
-    moved_store = pltpu.make_async_copy(moved_ref, moved_hbm, store_sem.at[6])
-    moved_store.start()
-    stores.append(moved_store)
-
-    with jax.named_scope("drain_mark"):
-        stores[0].wait()
+    for c in range(6):
+        samp_out[c] = samp[:, c, :]
+
     for j in range(len(CHUNKS)):
         for source, send_sem in ((out1, send1), (out2, send2)):
             sent = source.at[j, pl.ds(0, N - 1), pl.ds(0, len(CHUNKS[j]))]
             pltpu.make_async_copy(sent, sent, send_sem.at[j]).wait()
-    for store in stores[1:]:
-        store.wait()
+
+
+def finish(
+    stress_ref, seg, samp, field_ref, lbuf, second, third, stress_hbm, moved_hbm,
+    mbuf, second_buf, third_buf, moved_ref, store_sem,
+):
+    store = pltpu.make_async_copy(stress_ref, stress_hbm, store_sem.at[0])
+    store.start()
+    line = [seg[:, 3 + k, :] for k in range(3)]
+    burg = [seg[:, 6 + k, :] for k in range(3)]
+    start = [seg[:, k, :] for k in range(3)]
+    sampled = [samp[c] for c in range(6)]
+    second_buf[...] = second[...]
+    third_buf[...] = third[...]
+    mbuf[...] = jnp.zeros_like(mbuf)
+    with jax.named_scope("pair_second"):
+        position = advance(start, sampled, [field_ref[c] for c in range(6)], line, burg)
+        arms_into(mbuf, position, line, burg)
+        pair_blocks(position, lbuf, mbuf, second_buf, REST_SECOND)
+    with jax.named_scope("pair_third"):
+        position = advance(position, sampled, pair_field(position, second_buf), line, burg)
+        arms_into(mbuf, position, line, burg)
+        pair_blocks(position, lbuf, mbuf, third_buf, REST_THIRD)
+    with jax.named_scope("last"):
+        position = advance(position, sampled, pair_field(position, third_buf), line, burg)
+        for k in range(3):
+            moved_ref[k, 0] = position[k][HALO : HALO + CELLS] - start[k][HALO : HALO + CELLS]
+    moved_store = pltpu.make_async_copy(moved_ref, moved_hbm, store_sem.at[1])
+    moved_store.start()
+    store.wait()
+    moved_store.wait()
 
 
 def body(plastic, offsets, lines, burgers, counts, voxels):
@@ -453,14 +509,20 @@
     group = pltpu.VMEM((len(CHUNKS), N, 8, N), F32)
     vectors = pltpu.VMEM((3, 1, CELLS, N), F32)
     table, back = tables()
-    return pl.pallas_call(
+    vmem = pl.BlockSpec(memory_space=pltpu.VMEM)
+    state = pl.pallas_call(
         kernel,
         out_shape=(
-            jax.ShapeDtypeStruct((6, 16, 8, N), F32),
-            jax.ShapeDtypeStruct((3, 1, CELLS, N), F32),
+            pltpu.VMEM((6, 16, 8, N), F32),
+            pltpu.VMEM((WIDE, 16, N), F32),
+            pltpu.VMEM((6, WIDE, N), F32),
+            pltpu.VMEM((6, WIDE, N), F32),
+            pltpu.VMEM((WIDE, 16, N), F32),
+            pltpu.VMEM((WIDE, 32, N), F32),
+            pltpu.VMEM((WIDE, 32, N), F32),
         ),
         in_specs=[any_space] * 8,
-        out_specs=(any_space, any_space),
+        out_specs=(vmem,) * 7,
         scratch_shapes=[
             pltpu.VMEM((6, 16, 8, N), F32),
             pltpu.VMEM((10, 2 * N, 2 * N), BF16),
@@ -468,21 +530,37 @@
             vectors, vectors, vectors,
             pltpu.VMEM((1, CELLS), jnp.int32),
             pltpu.VMEM((1, CELLS, N), jnp.int32),
-            vectors,
             group, group, group, group,
             pltpu.VMEM((6, N, N), F32),
             pltpu.VMEM((6, N, N), F32),
             pltpu.VMEM((WIDE, 16, N), F32),
             pltpu.VMEM((WIDE, 8, N), F32),
-            pltpu.VMEM((WIDE, 16, N), F32),
+            pltpu.VMEM((WIDE, 8, N), F32),
             pltpu.VMEM((3, WIDE, 16, N), F32),
             pltpu.VMEM((WIDE, 32, N), F32),
+            pltpu.VMEM((CELLS, 2, N, N), F32),
             dma((17,)),
             dma((len(CHUNKS),)), dma((len(CHUNKS),)), dma((len(CHUNKS),)), dma((len(CHUNKS),)),
-            dma((2,)), dma((2,)), dma((2,)), dma((2,)), dma((7,)),
+            dma((2,)), dma((2,)), dma((2,)), dma((2,)),
         ],
         compiler_params=pltpu.CompilerParams(collective_id=0, has_side_effects=True),
     )(plastic, jnp.asarray(table), jnp.asarray(back), offsets, lines, burgers, counts, voxels)
+    return pl.pallas_call(
+        finish,
+        out_shape=(
+            jax.ShapeDtypeStruct((6, 16, 8, N), F32),
+            jax.ShapeDtypeStruct((3, 1, CELLS, N), F32),
+        ),
+        in_specs=[vmem] * 7,
+        out_specs=(any_space, any_space),
+        scratch_shapes=[
+            pltpu.VMEM((3, WIDE, 16, N), F32),
+            pltpu.VMEM((WIDE, 32, N), F32),
+            pltpu.VMEM((WIDE, 32, N), F32),
+            vectors,
+            dma((2,)),
+        ],
+    )(*[pltpu.with_memory_space_constraint(array, pltpu.VMEM) for array in state])
 
 
 def solution(mesh):

time: 38.6 us -> 34.6 us (0.90)
  local copies, waits for them, and re-layouts: 3.05 us -> 0 us
  Pallas kernels: 34.4 us -> 33.8 us
    unnamed x2 -> x0, local copies, waits for them, and re-layouts: 3.05 us -> none
    pallas_call x1 -> x2, Pallas kernels: 34.4 us -> 33.8 us  [the longest x1 31.6 us: body(): pl.pallas_call(kernel, out_shape=(pltpu.VMEM((6, 16, 8, N), F32), pltpu.V...]
where the time goes in v2:
time: 34.6 us; the launch traced here: 34.4 us
  Pallas kernels  33.8 us (98%)
  between operations  0.64 us (2%)
    pallas_call x1, Pallas kernels, body(): pl.pallas_call(kernel, out_shape=(pltpu.VMEM((6, 16, 8, N), F32), pltpu.V...  31.6 us
    pallas_call x1, Pallas kernels, body(): pl.pallas_call(finish, out_shape=(jax.ShapeDtypeStruct((6, 16, 8, N), F32...  2.14 us

profile of v2, /device:TPU:1, one launch (start us, length us, event | category | flops | bytes accessed | tf_op | source)
XLA Modules:
  0.0 34.4 jit_solution(15105039013592889466)
XLA Ops:
  0.6 31.6 %shard_map.95 = (f32[6,16,8,128]{3,2,1,0:T(8,128)S(1)}, f32[10,16,128]{2,1,0:T(8,128)S(1)}, f32[6,10,128]{2,1,0:T(8,128)S(1)}, f32[6,10,128]{2,1,0:T(8,128)S(1)}...) custom-call(f32[6,16,8,128]{3,2,1,0:T(8,128)} %plastic_hbm.1, ...), custom_call_target="tpu_custom_call" | custom-call | tf_op jit(solution)/shard_map/pallas_call | solution.py:513
  32.3 2.1 %shard_map.96 = (f32[6,16,8,128]{3,2,1,0:T(8,128)}, f32[3,1,4,128]{3,2,1,0:T(4,128)}) custom-call(f32[6,16,8,128]{3,2,1,0:T(8,128)S(1)} %get-tuple-element.9.stress_ref, f32[10,16,128]{2,1,0:T(8,128)S(1)} %get-tuple-element.10.seg, f32[6,10,128]{2,1,0:T(8,128)S(1)} %get-tuple-element.11.samp, f32[6,10,128]{2,1,0:T(8,128)S(1)} %get-tuple-element.12.field_ref, ...), custom_call_target="tpu_custom_call" | custom-call | tf_op jit(solution)/shard_map/pallas_call | solution.py:548

commit v3 on v2

--- a/solution.py
+++ b/solution.py
@@ -19,10 +19,11 @@
 CELLS = 4
 HALO = 3
 WIDE = CELLS + 2 * HALO
-OWN_SECOND = ((3, (1, 2), True), (4, (0, 1, 2), True), (5, (0, 1, 2), True), (6, (0, 1), True))
-REST_SECOND = ((2, (0, 1, 2), True), (3, (0,), False), (6, (2,), False), (7, (0, 1, 2), True))
-OWN_THIRD = ((4, (1, 2), True), (5, (0, 1), True))
-REST_THIRD = ((3, (0, 1, 2), True), (4, (0,), False), (5, (2,), False), (6, (0, 1, 2), True))
+LATE = 8
+OWN_SECOND = ((2, (1, 2)), (3, (0, 1, 2)), (4, (0, 1, 2)), (5, (0, 1)))
+REST_SECOND = ((1, (0, 1, 2)), (2, (0,)), (5, (2,)), (6, (0, 1, 2)))
+OWN_THIRD = ((3, (1, 2)), (4, (0, 1)))
+REST_THIRD = ((2, (0, 1, 2)), (3, (0,)), (4, (2,)), (5, (0, 1, 2)))
 
 lame_lambda = 1.5
 shear_modulus = 1.0
@@ -97,15 +98,19 @@
         for index in range(PA):
             if index & step == 0:
                 first, second = tiles[index], tiles[index + step]
-                tiles[index] = jnp.where(bit, pltpu.roll(second, step * 8, 1), first)
-                tiles[index + step] = jnp.where(bit, second, pltpu.roll(first, N - step * 8, 1))
+                going = jnp.where(bit, first, second)
+                if step * 8 == N // 2:
+                    gone = pltpu.roll(going, N // 2, 1)
+                else:
+                    gone = jnp.take_along_axis(going, lane ^ (step * 8), axis=1, mode="promise_in_bounds")
+                tiles[index] = jnp.where(bit, gone, first)
+                tiles[index + step] = jnp.where(bit, second, gone)
         step //= 2
     return jnp.concatenate(tiles, axis=0)
 
 
-def turned(value, upper):
-    other = pltpu.roll(value, N // 2, 1)
-    return jnp.where(upper, -other, other)
+def turned(value, sign):
+    return pltpu.roll(value, N // 2, 1) * sign
 
 
 def y_matmul(rows, table):
@@ -162,7 +167,7 @@
 
 
 def partners():
-    hops = (0, 1, 2, 1)
+    hops = (0.0, 1.0, 2.3, 1.6)
 
     def distance(i):
         low, high = i & 7, i >> 3
@@ -176,7 +181,14 @@
     return value.astype(F32)
 
 
+def row_of_cells(ref, row, first, count):
+    cells, rows = ref.shape[0], ref.shape[1]
+    return ref.reshape(cells * rows, N)[pl.ds(first * rows + row, count, stride=rows), :]
+
+
 def arms_into(mbuf, position, line, burg):
+    cells = position[0].shape[0]
+    flat = mbuf.reshape(3 * mbuf.shape[1] * 16, N)
     arm = [
         position[1] * line[2] - position[2] * line[1],
         position[2] * line[0] - position[0] * line[2],
@@ -190,13 +202,19 @@
         ]
         for a in range(3):
             for b in range(3):
-                mbuf[shift, :, 3 * a + b, :] = moved_arm[a] * burg[b]
-
-
-def pair_blocks(position, lbuf, mbuf, pair_out, blocks):
-    pad = jnp.zeros((16 - WIDE, N), F32)
-    columns = [jnp.transpose(jnp.concatenate([value, pad], axis=0)) for value in position]
-    for cell, shifts, fresh in blocks:
+                at = shift * mbuf.shape[1] * 16 + 3 * a + b
+                flat[pl.ds(at, cells, stride=16), :] = moved_arm[a] * burg[b]
+
+
+def pair_blocks(position, lbuf, mbuf, pair_out, blocks, before=None):
+    cells = position[0].shape[0]
+    extra = (WIDE - cells) // 2
+    if cells % 8:
+        pad = jnp.zeros((16 - cells, N), F32)
+        columns = [jnp.transpose(jnp.concatenate([value, pad], axis=0)) for value in position]
+    else:
+        columns = [jnp.transpose(value) for value in position]
+    for cell, shifts in blocks:
         target = [value[cell : cell + 1] for value in position]
         weights, factors = [], []
         for shift in shifts:
@@ -207,17 +225,20 @@
             radius = delta[0] * delta[0] + delta[1] * delta[1] + delta[2] * delta[2] + core_square
             root = lax.rsqrt(radius)
             weights.append(root * root * root)
-            factors.append(jnp.concatenate([lbuf[source], mbuf[shift, source]], axis=0))
+            factors.append(jnp.concatenate([lbuf[source + extra], mbuf[shift, source]], axis=0))
         weight_high, weight_low = split(jnp.concatenate(weights, axis=0))
         factor_high, factor_low = split(jnp.concatenate(factors, axis=1))
         both = dot(jnp.concatenate([factor_high, factor_low], axis=0), weight_high)
         total = both[:32] + both[32:] + dot(factor_high, weight_low)
-        pair_out[cell] = total if fresh else pair_out[cell] + total
+        if before is not None and len(shifts) < 3:
+            total = total + before[cell]
+        pair_out[cell] = total
 
 
 def pair_field(position, pair_out):
-    spread = [[pair_out[:, 3 * c + b, :] for b in range(3)] for c in range(3)]
-    offset = [[pair_out[:, 16 + 3 * a + b, :] for b in range(3)] for a in range(3)]
+    cells = position[0].shape[0]
+    spread = [[row_of_cells(pair_out, 3 * c + b, 0, cells) for b in range(3)] for c in range(3)]
+    offset = [[row_of_cells(pair_out, 16 + 3 * a + b, 0, cells) for b in range(3)] for a in range(3)]
     moment = [[None] * 3 for _ in range(3)]
     for b in range(3):
         for a in range(3):
@@ -244,7 +265,7 @@
     plastic_hbm, table_hbm, back_hbm, offsets_hbm, lines_hbm, burgers_hbm, counts_hbm, voxels_hbm,
     stress_out, seg_out, samp_out, field_out, lbuf, second_out, third_out,
     plastic_buf, table_buf, back_buf, offsets_ref, lines_ref, burgers_ref, counts_ref, voxels_ref,
-    out1, in1, out2, in2, spec, stress_buf, seg, samp, own, mbuf, pair_out, factor_buf,
+    out1, in1, out2, in2, spec, stress_buf, seg, samp, own, mbuf, mlate, pair_out, factor_buf,
     load_sem, send1, recv1, send2, recv2, halo_send, halo_recv, samp_send, samp_recv,
 ):
     gx = lax.axis_index("gx")
@@ -277,7 +298,7 @@
             copy.start()
 
     lane8 = lax.broadcasted_iota(jnp.int32, (8, N), 1)
-    upper = lax.broadcasted_iota(jnp.int32, (N, N), 1) >= N // 2
+    upper = jnp.where(lax.broadcasted_iota(jnp.int32, (N, N), 1) >= N // 2, -1.0, 1.0)
 
     def send_all(j, source, target, send_sem, recv_sem):
         rows = pl.ds(0, len(CHUNKS[j]))
@@ -379,23 +400,25 @@
     with jax.named_scope("wait_halo"):
         to_left.wait()
         to_right.wait()
-    line = [seg[:, 3 + k, :] for k in range(3)]
-    burg = [seg[:, 6 + k, :] for k in range(3)]
-    start = [seg[:, k, :] for k in range(3)]
-    seg_out[...] = seg[...]
+    start, line, burg = ([row_of_cells(seg, 3 * i + k, 0, WIDE) for k in range(3)] for i in range(3))
+    for i, part in enumerate((start, line, burg)):
+        for k in range(3):
+            seg_out[3 * i + k] = part[k][1 : 1 + LATE]
     with jax.named_scope("pair1"):
         lbuf[...] = jnp.zeros_like(lbuf)
         mbuf[...] = jnp.zeros_like(mbuf)
+        mlate[...] = jnp.zeros_like(mlate)
         pair_out[...] = jnp.zeros_like(pair_out)
         own[...] = jnp.zeros_like(own)
+        flat = lbuf.reshape(WIDE * 16, N)
         for c in range(3):
             for b in range(3):
-                lbuf[:, 3 * c + b, :] = line[c] * burg[b]
+                flat[pl.ds(3 * c + b, WIDE, stride=16), :] = line[c] * burg[b]
         arms_into(mbuf, start, line, burg)
-        pair_blocks(start, lbuf, mbuf, pair_out, [(cell, (0, 1, 2), True) for cell in range(1, WIDE - 1)])
+        pair_blocks(start, lbuf, mbuf, pair_out, [(cell, (0, 1, 2)) for cell in range(1, WIDE - 1)])
         field = pair_field(start, pair_out)
         for c in range(6):
-            field_out[c] = field[c]
+            field_out[c] = field[c][1 : 1 + LATE]
         second_out[...] = jnp.zeros_like(second_out)
         third_out[...] = jnp.zeros_like(third_out)
 
@@ -451,20 +474,20 @@
             for c, half in zip(pair, (result[:, :N], result[:, N:])):
                 stress_out[c] = jnp.transpose(half).reshape(16, 8, N)
     with jax.named_scope("pair_own"):
-        position = advance(start, [own[:, c, :] for c in range(6)], field, line, burg)
-        arms_into(mbuf, position, line, burg)
-        pair_blocks(position, lbuf, mbuf, second_out, OWN_SECOND)
-        position = advance(
-            position, [own[:, c, :] for c in range(6)], pair_field(position, second_out), line, burg
-        )
-        arms_into(mbuf, position, line, burg)
-        pair_blocks(position, lbuf, mbuf, third_out, OWN_THIRD)
+        start, line, burg = ([seg_out[3 * i + k] for k in range(3)] for i in range(3))
+        sampled = [row_of_cells(own, c, 1, LATE) for c in range(6)]
+        position = advance(start, sampled, [field_out[c] for c in range(6)], line, burg)
+        arms_into(mlate, position, line, burg)
+        pair_blocks(position, lbuf, mlate, second_out, OWN_SECOND)
+        position = advance(position, sampled, pair_field(position, second_out), line, burg)
+        arms_into(mlate, position, line, burg)
+        pair_blocks(position, lbuf, mlate, third_out, OWN_THIRD)
 
     with jax.named_scope("wait_samp"):
         samp_left.wait()
         samp_right.wait()
     for c in range(6):
-        samp_out[c] = samp[:, c, :]
+        samp_out[c] = row_of_cells(samp, c, 1, LATE)
 
     for j in range(len(CHUNKS)):
         for source, send_sem in ((out1, send1), (out2, send2)):
@@ -478,25 +501,24 @@
 ):
     store = pltpu.make_async_copy(stress_ref, stress_hbm, store_sem.at[0])
     store.start()
-    line = [seg[:, 3 + k, :] for k in range(3)]
-    burg = [seg[:, 6 + k, :] for k in range(3)]
-    start = [seg[:, k, :] for k in range(3)]
+    start, line, burg = ([seg[3 * i + k] for k in range(3)] for i in range(3))
     sampled = [samp[c] for c in range(6)]
-    second_buf[...] = second[...]
-    third_buf[...] = third[...]
-    mbuf[...] = jnp.zeros_like(mbuf)
+    for cell in (0, 3, 4, 7):
+        second_buf[cell] = second[cell]
+    for cell in (0, 1, 6, 7):
+        third_buf[cell] = third[cell]
     with jax.named_scope("pair_second"):
         position = advance(start, sampled, [field_ref[c] for c in range(6)], line, burg)
         arms_into(mbuf, position, line, burg)
-        pair_blocks(position, lbuf, mbuf, second_buf, REST_SECOND)
+        pair_blocks(position, lbuf, mbuf, second_buf, REST_SECOND, second)
     with jax.named_scope("pair_third"):
         position = advance(position, sampled, pair_field(position, second_buf), line, burg)
         arms_into(mbuf, position, line, burg)
-        pair_blocks(position, lbuf, mbuf, third_buf, REST_THIRD)
+        pair_blocks(position, lbuf, mbuf, third_buf, REST_THIRD, third)
     with jax.named_scope("last"):
         position = advance(position, sampled, pair_field(position, third_buf), line, burg)
         for k in range(3):
-            moved_ref[k, 0] = position[k][HALO : HALO + CELLS] - start[k][HALO : HALO + CELLS]
+            moved_ref[k, 0] = (position[k] - start[k])[2 : 2 + CELLS]
     moved_store = pltpu.make_async_copy(moved_ref, moved_hbm, store_sem.at[1])
     moved_store.start()
     store.wait()
@@ -514,12 +536,12 @@
         kernel,
         out_shape=(
             pltpu.VMEM((6, 16, 8, N), F32),
+            pltpu.VMEM((9, LATE, N), F32),
+            pltpu.VMEM((6, LATE, N), F32),
+            pltpu.VMEM((6, LATE, N), F32),
             pltpu.VMEM((WIDE, 16, N), F32),
-            pltpu.VMEM((6, WIDE, N), F32),
-            pltpu.VMEM((6, WIDE, N), F32),
-            pltpu.VMEM((WIDE, 16, N), F32),
-            pltpu.VMEM((WIDE, 32, N), F32),
-            pltpu.VMEM((WIDE, 32, N), F32),
+            pltpu.VMEM((LATE, 32, N), F32),
+            pltpu.VMEM((LATE, 32, N), F32),
         ),
         in_specs=[any_space] * 8,
         out_specs=(vmem,) * 7,
@@ -537,6 +559,7 @@
             pltpu.VMEM((WIDE, 8, N), F32),
             pltpu.VMEM((WIDE, 8, N), F32),
             pltpu.VMEM((3, WIDE, 16, N), F32),
+            pltpu.VMEM((3, LATE, 16, N), F32),
             pltpu.VMEM((WIDE, 32, N), F32),
             pltpu.VMEM((CELLS, 2, N, N), F32),
             dma((17,)),
@@ -554,9 +577,9 @@
         in_specs=[vmem] * 7,
         out_specs=(any_space, any_space),
         scratch_shapes=[
-            pltpu.VMEM((3, WIDE, 16, N), F32),
-            pltpu.VMEM((WIDE, 32, N), F32),
-            pltpu.VMEM((WIDE, 32, N), F32),
+            pltpu.VMEM((3, LATE, 16, N), F32),
+            pltpu.VMEM((LATE, 32, N), F32),
+            pltpu.VMEM((LATE, 32, N), F32),
             vectors,
             dma((2,)),
         ],

time: 34.6 us -> 33.7 us (0.974)
  Pallas kernels: 33.8 us -> 32.9 us
    pallas_call x1, Pallas kernels: 31.6 us -> 30.8 us  [body(): pl.pallas_call(kernel, out_shape=(pltpu.VMEM((6, 16, 8, N), F32), pltpu.V...]
where the time goes in v3:
time: 33.7 us; the launch traced here: 33.5 us
  Pallas kernels  32.9 us (98%)
  between operations  0.64 us (2%)
    pallas_call x1, Pallas kernels, body(): pl.pallas_call(kernel, out_shape=(pltpu.VMEM((6, 16, 8, N), F32), pltpu.V...  30.8 us
    pallas_call x1, Pallas kernels, body(): pl.pallas_call(finish, out_shape=(jax.ShapeDtypeStruct((6, 16, 8, N), F32...  2.09 us

profile of v3, /device:TPU:1, one launch (start us, length us, event | category | flops | bytes accessed | tf_op | source)
XLA Modules:
  0.0 33.5 jit_solution(5588180440455658537)
XLA Ops:
  0.6 30.8 %shard_map.95 = (f32[6,16,8,128]{3,2,1,0:T(8,128)S(1)}, f32[9,8,128]{2,1,0:T(8,128)S(1)}, f32[6,8,128]{2,1,0:T(8,128)S(1)}, f32[6,8,128]{2,1,0:T(8,128)S(1)}, f3...) custom-call(f32[6,16,8,128]{3,2,1,0:T(8,128)} %plastic_hbm.1, ...), custom_call_target="tpu_custom_call" | custom-call | tf_op jit(solution)/shard_map/pallas_call | solution.py:535
  31.5 2.1 %shard_map.96 = (f32[6,16,8,128]{3,2,1,0:T(8,128)}, f32[3,1,4,128]{3,2,1,0:T(4,128)}) custom-call(f32[6,16,8,128]{3,2,1,0:T(8,128)S(1)} %get-tuple-element.9.stress_ref, f32[9,8,128]{2,1,0:T(8,128)S(1)} %get-tuple-element.10.seg, f32[6,8,128]{2,1,0:T(8,128)S(1)} %get-tuple-element.11.samp, f32[6,8,128]{2,1,0:T(8,128)S(1)} %get-tuple-element.12.field_ref, ...), custom_call_target="tpu_custom_call" | custom-call | tf_op jit(solution)/shard_map/pallas_call | solution.py:571

commit v4 on v3

--- a/solution.py
+++ b/solution.py
@@ -14,7 +14,6 @@
 N = 128
 GX = 8
 PA = 16
-CHUNKS = ((0, 1, 2, 5, 3, 4),)
 PAIRS = ((0, 1), (2, 5), (3, 4))
 CELLS = 4
 HALO = 3
@@ -273,7 +272,6 @@
     mode = pa * GX + gx
     left = {"gx": (gx + 7) % 8}
     right = {"gx": (gx + 1) % 8}
-    place = {c: (j, row) for j, chunk in enumerate(CHUNKS) for row, c in enumerate(chunk)}
 
     def device(i):
         return {"gx": gx ^ (i & 7), "pa": pa ^ (i >> 3)}
@@ -300,27 +298,25 @@
     lane8 = lax.broadcasted_iota(jnp.int32, (8, N), 1)
     upper = jnp.where(lax.broadcasted_iota(jnp.int32, (N, N), 1) >= N // 2, -1.0, 1.0)
 
-    def send_all(j, source, target, send_sem, recv_sem):
-        rows = pl.ds(0, len(CHUNKS[j]))
+    def message(ref, number):
+        return ref.at[pl.ds(6 * number, 6)]
+
+    def send_all(source, target, send_sem, recv_sem):
         for i in partners():
             pltpu.make_async_remote_copy(
-                src_ref=source.at[j, mode ^ i, rows], dst_ref=target.at[j, mode, rows],
-                send_sem=send_sem.at[j], recv_sem=recv_sem.at[j],
-                device_id=device(i), device_id_type=MESH,
+                src_ref=message(source, mode ^ i), dst_ref=message(target, mode),
+                send_sem=send_sem, recv_sem=recv_sem, device_id=device(i), device_id_type=MESH,
             ).start()
-        pltpu.make_async_copy(source.at[j, mode, rows], target.at[j, mode, rows], recv_sem.at[j]).start()
-
-    def wait_all(j, target, recv_sem):
-        whole = target.at[j, :, pl.ds(0, len(CHUNKS[j]))]
-        pltpu.make_async_copy(whole, whole, recv_sem.at[j]).wait()
+        pltpu.make_async_copy(message(source, mode), message(target, mode), recv_sem).start()
+
+    def wait_all(target, recv_sem):
+        pltpu.make_async_copy(target, target, recv_sem).wait()
 
     def put(target, c, value):
-        j, row = place[c]
-        target.reshape(len(CHUNKS) * N * 8, N)[pl.ds(j * N * 8 + row, N, stride=8), :] = value
+        target[pl.ds(c, N, stride=6), :] = value
 
     def take(source, c):
-        j, row = place[c]
-        return source.reshape(len(CHUNKS) * N * 8, N)[pl.ds(j * N * 8 + row, N, stride=8), :]
+        return source[pl.ds(c, N, stride=6), :]
 
     with jax.named_scope("wait_load"):
         loads[0].wait()
@@ -337,8 +333,7 @@
     with jax.named_scope("wait_barrier"):
         pl.semaphore_wait(barrier, N - 1)
     with jax.named_scope("send1"):
-        for j in range(len(CHUNKS)):
-            send_all(j, out1, in1, send1, recv1)
+        send_all(out1, in1, send1, recv1)
 
     for copy in loads[1:6]:
         copy.wait()
@@ -365,12 +360,11 @@
     for copy in table_loads[2:]:
         copy.wait()
     loads[6].wait()
-    for j in range(len(CHUNKS)):
-        with jax.named_scope("wait_in1"):
-            wait_all(j, in1, recv1)
-        with jax.named_scope("y_ahead"):
-            for c in CHUNKS[j]:
-                spec[c] = y_matmul(butterfly(take(in1, c), lane8), table_buf[2])
+    with jax.named_scope("wait_in1"):
+        wait_all(in1, recv1)
+    with jax.named_scope("y_ahead"):
+        for c in range(6):
+            spec[c] = y_matmul(butterfly(take(in1, c), lane8), table_buf[2])
     with jax.named_scope("x_ahead"):
         for pair in PAIRS:
             table = table_buf[4 if pair[0] == 3 else 3]
@@ -390,12 +384,11 @@
         for pair in PAIRS:
             table = table_buf[6 if pair[0] == 3 else 5]
             spec[pair[0]], spec[pair[1]] = x_matmul(table, spec[pair[0]], spec[pair[1]], upper)
-    for j in range(len(CHUNKS)):
-        with jax.named_scope("y_back"):
-            for c in CHUNKS[j]:
-                put(out2, c, butterfly(y_matmul(spec[c], table_buf[7]), lane8))
-        with jax.named_scope("send2"):
-            send_all(j, out2, in2, send2, recv2)
+    with jax.named_scope("y_back"):
+        for c in range(6):
+            put(out2, c, butterfly(y_matmul(spec[c], table_buf[7]), lane8))
+    with jax.named_scope("send2"):
+        send_all(out2, in2, send2, recv2)
 
     with jax.named_scope("wait_halo"):
         to_left.wait()
@@ -434,9 +427,8 @@
                     factor_buf[cell, odd, rows] = jnp.take_along_axis(
                         back_buf[odd, rows], pick_z, axis=1, mode="promise_in_bounds"
                     )
-    for j in range(len(CHUNKS)):
-        with jax.named_scope("wait_in2"):
-            wait_all(j, in2, recv2)
+    with jax.named_scope("wait_in2"):
+        wait_all(in2, recv2)
     with jax.named_scope("sample"):
         for c in range(6):
             stress_buf[c] = take(in2, c)
@@ -489,10 +481,9 @@
     for c in range(6):
         samp_out[c] = row_of_cells(samp, c, 1, LATE)
 
-    for j in range(len(CHUNKS)):
-        for source, send_sem in ((out1, send1), (out2, send2)):
-            sent = source.at[j, pl.ds(0, N - 1), pl.ds(0, len(CHUNKS[j]))]
-            pltpu.make_async_copy(sent, sent, send_sem.at[j]).wait()
+    for source, send_sem in ((out1, send1), (out2, send2)):
+        sent = source.at[pl.ds(0, 6 * (N - 1))]
+        pltpu.make_async_copy(sent, sent, send_sem).wait()
 
 
 def finish(
@@ -528,7 +519,7 @@
 def body(plastic, offsets, lines, burgers, counts, voxels):
     any_space = pl.BlockSpec(memory_space=pl.ANY)
     dma = pltpu.SemaphoreType.DMA
-    group = pltpu.VMEM((len(CHUNKS), N, 8, N), F32)
+    group = pltpu.VMEM((6 * N, N), F32)
     vectors = pltpu.VMEM((3, 1, CELLS, N), F32)
     table, back = tables()
     vmem = pl.BlockSpec(memory_space=pltpu.VMEM)
@@ -563,7 +554,7 @@
             pltpu.VMEM((WIDE, 32, N), F32),
             pltpu.VMEM((CELLS, 2, N, N), F32),
             dma((17,)),
-            dma((len(CHUNKS),)), dma((len(CHUNKS),)), dma((len(CHUNKS),)), dma((len(CHUNKS),)),
+            dma, dma, dma, dma,
             dma((2,)), dma((2,)), dma((2,)), dma((2,)),
         ],
         compiler_params=pltpu.CompilerParams(collective_id=0, has_side_effects=True),

time: 33.7 us -> 33.7 us (level)
  no operation moved by 1% of the time
where the time goes in v4:
time: 33.7 us; the launch traced here: 33.6 us
  Pallas kernels  33 us (98%)
  between operations  0.64 us (2%)
    pallas_call x1, Pallas kernels, body(): pl.pallas_call(kernel, out_shape=(pltpu.VMEM((6, 16, 8, N), F32), pltpu.V...  30.9 us
    pallas_call x1, Pallas kernels, body(): pl.pallas_call(finish, out_shape=(jax.ShapeDtypeStruct((6, 16, 8, N), F32...  2.09 us

profile of v4, /device:TPU:1, one launch (start us, length us, event | category | flops | bytes accessed | tf_op | source)
XLA Modules:
  0.0 33.6 jit_solution(11642832005070800938)
XLA Ops:
  0.6 30.9 %shard_map.95 = (f32[6,16,8,128]{3,2,1,0:T(8,128)S(1)}, f32[9,8,128]{2,1,0:T(8,128)S(1)}, f32[6,8,128]{2,1,0:T(8,128)S(1)}, f32[6,8,128]{2,1,0:T(8,128)S(1)}, f3...) custom-call(f32[6,16,8,128]{3,2,1,0:T(8,128)} %plastic_hbm.1, ...), custom_call_target="tpu_custom_call" | custom-call | tf_op jit(solution)/shard_map/pallas_call | solution.py:526
  31.5 2.1 %shard_map.96 = (f32[6,16,8,128]{3,2,1,0:T(8,128)}, f32[3,1,4,128]{3,2,1,0:T(4,128)}) custom-call(f32[6,16,8,128]{3,2,1,0:T(8,128)S(1)} %get-tuple-element.9.stress_ref, f32[9,8,128]{2,1,0:T(8,128)S(1)} %get-tuple-element.10.seg, f32[6,8,128]{2,1,0:T(8,128)S(1)} %get-tuple-element.11.samp, f32[6,8,128]{2,1,0:T(8,128)S(1)} %get-tuple-element.12.field_ref, ...), custom_call_target="tpu_custom_call" | custom-call | tf_op jit(solution)/shard_map/pallas_call | solution.py:562

commit v5 on v4

--- a/solution.py
+++ b/solution.py
@@ -91,20 +91,26 @@
 
 def butterfly(value, lane):
     tiles = [value[8 * t : 8 * t + 8] for t in range(PA)]
-    step = PA // 2
-    while step >= 1:
-        bit = (lane & (step * 8)) != 0
-        for index in range(PA):
-            if index & step == 0:
-                first, second = tiles[index], tiles[index + step]
-                going = jnp.where(bit, first, second)
-                if step * 8 == N // 2:
-                    gone = pltpu.roll(going, N // 2, 1)
+    for step in (4, 1):
+        low = (lane & (step * 8)) != 0
+        high = (lane & (step * 16)) != 0
+
+        def by_digit(options):
+            return jnp.where(high, jnp.where(low, options[3], options[2]), jnp.where(low, options[1], options[0]))
+
+        for base in range(PA):
+            if base & (3 * step):
+                continue
+            held = [tiles[base + step * t] for t in range(4)]
+            gone = [None] * 4
+            for d in range(1, 4):
+                going = by_digit([held[u ^ d] for u in range(4)])
+                if d * step * 8 == N // 2:
+                    gone[d] = pltpu.roll(going, N // 2, 1)
                 else:
-                    gone = jnp.take_along_axis(going, lane ^ (step * 8), axis=1, mode="promise_in_bounds")
-                tiles[index] = jnp.where(bit, gone, first)
-                tiles[index + step] = jnp.where(bit, second, gone)
-        step //= 2
+                    gone[d] = jnp.take_along_axis(going, lane ^ (d * step * 8), axis=1, mode="promise_in_bounds")
+            for t in range(4):
+                tiles[base + step * t] = by_digit([held[t] if g == t else gone[g ^ t] for g in range(4)])
     return jnp.concatenate(tiles, axis=0)
 
 
@@ -165,12 +171,13 @@
     )
 
 
-def partners():
-    hops = (0.0, 1.0, 2.3, 1.6)
-
+SEND_COST = ((0.0, 0.6, 1.5, 1.0), (0.0, 1.0, 2.3, 1.6), (0.0, 1.5, 3.6, 2.4))
+GREET_COST = ((0.0, 1.0, 2.0, 2.4),) * 3
+
+
+def partners(cost):
     def distance(i):
-        low, high = i & 7, i >> 3
-        return hops[2 * (high >> 3) + (low & 1)] + hops[low >> 1] + hops[(high >> 1) & 3]
+        return cost[0][2 * (i >> 6) + (i & 1)] + cost[1][(i & 7) >> 1] + cost[2][(i >> 4) & 3]
 
     return sorted(range(1, N), key=lambda i: -distance(i))
 
@@ -290,7 +297,7 @@
         loads[0].start()
         table_loads[0].start()
         table_loads[1].start()
-        for i in partners():
+        for i in partners(GREET_COST):
             pl.semaphore_signal(barrier, inc=1, device_id=device(i), device_id_type=MESH)
         for copy in loads[1:] + table_loads[2:]:
             copy.start()
@@ -302,7 +309,7 @@
         return ref.at[pl.ds(6 * number, 6)]
 
     def send_all(source, target, send_sem, recv_sem):
-        for i in partners():
+        for i in partners(SEND_COST):
             pltpu.make_async_remote_copy(
                 src_ref=message(source, mode ^ i), dst_ref=message(target, mode),
                 send_sem=send_sem, recv_sem=recv_sem, device_id=device(i), device_id_type=MESH,

time: 33.7 us -> 33.2 us (0.985)
  Pallas kernels: 33 us -> 32.3 us
    pallas_call x1, Pallas kernels: 30.9 us -> 30.2 us  [body(): pl.pallas_call(kernel, out_shape=(pltpu.VMEM((6, 16, 8, N), F32), pltpu.V...]
where the time goes in v5:
time: 33.2 us; the launch traced here: 32.9 us
  Pallas kernels  32.3 us (97%)
  between operations  0.64 us (2%)
    pallas_call x1, Pallas kernels, body(): pl.pallas_call(kernel, out_shape=(pltpu.VMEM((6, 16, 8, N), F32), pltpu.V...  30.2 us
    pallas_call x1, Pallas kernels, body(): pl.pallas_call(finish, out_shape=(jax.ShapeDtypeStruct((6, 16, 8, N), F32...  2.09 us

profile of v5, /device:TPU:1, one launch (start us, length us, event | category | flops | bytes accessed | tf_op | source)
XLA Modules:
  0.0 32.9 jit_solution(2548016317232640535)
XLA Ops:
  0.6 30.2 %shard_map.95 = (f32[6,16,8,128]{3,2,1,0:T(8,128)S(1)}, f32[9,8,128]{2,1,0:T(8,128)S(1)}, f32[6,8,128]{2,1,0:T(8,128)S(1)}, f32[6,8,128]{2,1,0:T(8,128)S(1)}, f3...) custom-call(f32[6,16,8,128]{3,2,1,0:T(8,128)} %plastic_hbm.1, ...), custom_call_target="tpu_custom_call" | custom-call | tf_op jit(solution)/shard_map/pallas_call | solution.py:533
  30.9 2.1 %shard_map.96 = (f32[6,16,8,128]{3,2,1,0:T(8,128)}, f32[3,1,4,128]{3,2,1,0:T(4,128)}) custom-call(f32[6,16,8,128]{3,2,1,0:T(8,128)S(1)} %get-tuple-element.9.stress_ref, f32[9,8,128]{2,1,0:T(8,128)S(1)} %get-tuple-element.10.seg, f32[6,8,128]{2,1,0:T(8,128)S(1)} %get-tuple-element.11.samp, f32[6,8,128]{2,1,0:T(8,128)S(1)} %get-tuple-element.12.field_ref, ...), custom_call_target="tpu_custom_call" | custom-call | tf_op jit(solution)/shard_map/pallas_call | solution.py:569

commit v6 on v5

--- a/solution.py
+++ b/solution.py
@@ -423,7 +423,6 @@
         third_out[...] = jnp.zeros_like(third_out)
 
     voxels = voxels_ref[0]
-    column_of = voxels >> 7
     z_of = voxels & 127
     with jax.named_scope("factors"):
         for cell in range(CELLS):
@@ -439,31 +438,35 @@
     with jax.named_scope("sample"):
         for c in range(6):
             stress_buf[c] = take(in2, c)
-        for cell in range(CELLS):
-            pick = jnp.broadcast_to(column_of[cell : cell + 1], (8, N))
-            total = [None] * 6
-            for t in range(N // 8):
-                rows = slice(8 * t, 8 * t + 8)
-                factor = [factor_buf[cell, odd, rows] for odd in range(2)]
+        near_side = gx % 2
+        first = 2 * near_side
+        far_slot = HALO + CELLS - (HALO + CELLS - 1) * near_side
+        copies = []
+        for half in range(2):
+            begin = first if half == 0 else 2 - first
+            for k in range(2):
+                cell = begin + k
+                pick = jnp.broadcast_to(voxels_ref[0, pl.ds(cell, 1), :] >> 7, (8, N))
+                total = [None] * 6
+                for t in range(N // 8):
+                    rows = slice(8 * t, 8 * t + 8)
+                    factor = [factor_buf[cell, odd, rows] for odd in range(2)]
+                    for c in range(6):
+                        tile = jnp.take_along_axis(stress_buf[c, rows], pick, axis=1, mode="promise_in_bounds")
+                        term = tile * factor[1 if c in (3, 4) else 0]
+                        total[c] = term if t == 0 else total[c] + term
                 for c in range(6):
-                    tile = jnp.take_along_axis(stress_buf[c, rows], pick, axis=1, mode="promise_in_bounds")
-                    term = tile * factor[1 if c in (3, 4) else 0]
-                    total[c] = term if t == 0 else total[c] + term
-            for c in range(6):
-                value = jnp.sum(total[c], axis=0, keepdims=True)
-                samp[HALO + cell, c : c + 1, :] = value
-                own[HALO + cell, c : c + 1, :] = value
-
-    samp_left = pltpu.make_async_remote_copy(
-        src_ref=samp.at[pl.ds(HALO, 2)], dst_ref=samp.at[pl.ds(HALO + CELLS, 2)],
-        send_sem=samp_send.at[0], recv_sem=samp_recv.at[0], device_id=left, device_id_type=MESH,
-    )
-    samp_right = pltpu.make_async_remote_copy(
-        src_ref=samp.at[pl.ds(HALO + 2, 2)], dst_ref=samp.at[pl.ds(1, 2)],
-        send_sem=samp_send.at[1], recv_sem=samp_recv.at[1], device_id=right, device_id_type=MESH,
-    )
-    samp_left.start()
-    samp_right.start()
+                    value = jnp.sum(total[c], axis=0, keepdims=True)
+                    samp[HALO + cell, c : c + 1, :] = value
+                    own[HALO + cell, c : c + 1, :] = value
+            other = (gx + 7 + 2 * near_side) % 8 if half == 0 else gx + 1 - 2 * near_side
+            slot = far_slot if half == 0 else HALO + CELLS + 1 - far_slot
+            copy = pltpu.make_async_remote_copy(
+                src_ref=samp.at[pl.ds(HALO + begin, 2)], dst_ref=samp.at[pl.ds(slot, 2)],
+                send_sem=samp_send.at[half], recv_sem=samp_recv.at[half], device_id={"gx": other}, device_id_type=MESH,
+            )
+            copy.start()
+            copies.append(copy)
     with jax.named_scope("z_back"):
         for pair in PAIRS:
             table = table_buf[9 if pair[0] == 3 else 8]
@@ -483,8 +486,8 @@
         pair_blocks(position, lbuf, mlate, third_out, OWN_THIRD)
 
     with jax.named_scope("wait_samp"):
-        samp_left.wait()
-        samp_right.wait()
+        for copy in copies:
+            copy.wait()
     for c in range(6):
         samp_out[c] = row_of_cells(samp, c, 1, LATE)
 

time: 33.2 us -> 32.9 us (level)
  no operation moved by 1% of the time
where the time goes in v6:
time: 32.9 us; the launch traced here: 32.7 us
  Pallas kernels  32 us (97%)
  between operations  0.64 us (2%)
    pallas_call x1, Pallas kernels, body(): pl.pallas_call(kernel, out_shape=(pltpu.VMEM((6, 16, 8, N), F32), pltpu.V...  29.9 us
    pallas_call x1, Pallas kernels, body(): pl.pallas_call(finish, out_shape=(jax.ShapeDtypeStruct((6, 16, 8, N), F32...  2.09 us

profile of v6, /device:TPU:1, one launch (start us, length us, event | category | flops | bytes accessed | tf_op | source)
XLA Modules:
  0.0 32.7 jit_solution(5233020574664082905)
XLA Ops:
  0.6 29.9 %shard_map.95 = (f32[6,16,8,128]{3,2,1,0:T(8,128)S(1)}, f32[9,8,128]{2,1,0:T(8,128)S(1)}, f32[6,8,128]{2,1,0:T(8,128)S(1)}, f32[6,8,128]{2,1,0:T(8,128)S(1)}, f3...) custom-call(f32[6,16,8,128]{3,2,1,0:T(8,128)} %plastic_hbm.1, ...), custom_call_target="tpu_custom_call" | custom-call | tf_op jit(solution)/shard_map/pallas_call | solution.py:536
  30.6 2.1 %shard_map.96 = (f32[6,16,8,128]{3,2,1,0:T(8,128)}, f32[3,1,4,128]{3,2,1,0:T(4,128)}) custom-call(f32[6,16,8,128]{3,2,1,0:T(8,128)S(1)} %get-tuple-element.9.stress_ref, f32[9,8,128]{2,1,0:T(8,128)S(1)} %get-tuple-element.10.seg, f32[6,8,128]{2,1,0:T(8,128)S(1)} %get-tuple-element.11.samp, f32[6,8,128]{2,1,0:T(8,128)S(1)} %get-tuple-element.12.field_ref, ...), custom_call_target="tpu_custom_call" | custom-call | tf_op jit(solution)/shard_map/pallas_call | solution.py:572
